TPU v7x, 32 devices: a whole 2x2x4 slice. The times are simulated.
32 devices in a mesh: dp: 32 (over z, y, x, core), feat: 1.
Axes of the slice: x: 2, y: 2, z: 4, core: 2. Of those that a mesh axis runs over, the one named last changes fastest.
Arguments:
- grads: bfloat16 [16384, 4096], P('dp', 'feat'), may hold values from -6 to 6
- covariance: float32 [4096, 4096], P('dp', 'feat'), may hold values from -0.16 to 6, as said below
- test_grads: bfloat16 [512, 4096], P('feat', 'dp'), may hold values from -0.09375 to 0.09375
- inverse_factor: bfloat16 [4096, 4096], P('dp'), may hold values from -0.09375 to 0.09375
Outputs:
- scores: float32 [16384, 512], P('dp', 'feat')
- covariance_out: float32 [4096, 4096], P('dp', 'feat')
Inputs may be any that keep to these rules, and one draw needn't show every extreme that they name: covariance is symmetric.
All inputs are finite; a program needn't handle non-finite values.
Results may differ from a plain program's by a relative error of at most 0.0029.
Values may be sent and summed in bfloat16 or wider, within the bound.
A program may use at most 256 MiB of HBM per device.

v0:
```python
import functools

import jax
import jax.numpy as jnp
from jax import lax
from jax.experimental import pallas as pl
from jax.experimental.pallas import tpu as pltpu
from jax.sharding import PartitionSpec as P

F32 = jnp.float32
BF16 = jnp.bfloat16
MESH = pl.DeviceIdType.MESH


def general(grads, covariance, test_grads, inverse_factor):
    all_features = lax.all_gather(grads, "feat", axis=1, tiled=True)
    examples = grads.shape[0] * lax.axis_size("dp")
    tested = lax.dot_general(
        inverse_factor, test_grads, (((0,), (1,)), ((), ())), preferred_element_type=F32
    )
    term = lax.dot_general(
        all_features, grads, (((0,), (0,)), ((), ())), preferred_element_type=F32
    )
    joined = lax.psum_scatter(
        jnp.concatenate([term, tested], axis=1), "dp", scatter_dimension=0, tiled=True
    )
    width = grads.shape[1]
    owned_pre = joined[:, width:].astype(BF16)
    pre_columns = lax.all_gather(owned_pre, "dp", axis=0, tiled=True)
    scores = jnp.dot(all_features, pre_columns, preferred_element_type=F32)
    return scores, 0.9 * covariance + joined[:, :width] / examples


class Sizes:
    def __init__(self, n, rows, k, tests):
        self.n, self.rows, self.k, self.tests = n, rows, k, tests
        self.chips, self.far, self.w = n // 2, n // 8, k // n
        self.W = 2 * self.w
        self.half = self.chips // 2
        self.each = self.half // 2
        self.ra = self.each // 2 * self.W
        self.rb = (self.each - self.each // 2) * self.W + self.w // 2
        self.mh = tests // 2

    def scratch(self):
        far, w, W, tests = self.far, self.w, self.W, self.tests
        far1 = max(far - 1, 1)
        v = pltpu.VMEM
        return dict(
            gbuf=v((2 * self.rows, self.k), BF16),
            gt=v((W, 2 * self.rows), BF16),
            tmp=v((self.ra + self.rb, W), F32),
            part_a=v((far, 2, self.ra, W), F32),
            part_b=v((far, 2, self.rb, W), F32),
            out_a1=v((far, 2, self.ra, W), BF16),
            out_b1=v((far, 2, self.rb, W), BF16),
            in_a1=v((far, 2, self.ra, W), BF16),
            in_b1=v((far, 2, self.rb, W), BF16),
            out_a2=v((far, self.ra, W), BF16),
            out_b2=v((far, self.rb, W), BF16),
            in_a2=v((far, self.ra, W), BF16),
            in_b2=v((far, self.rb, W), BF16),
            out_az=v((far1, self.ra, W), BF16),
            out_bz=v((far1, self.rb, W), BF16),
            in_az=v((far1, self.ra, W), BF16),
            in_bz=v((far1, self.rb, W), BF16),
            fbuf=v((2 * far * w, 4 * w), BF16),
            tbuf=v((tests, 2 * far * w), BF16),
            pp=v((tests, 4 * w), F32),
            in_p1=v((2, 2, self.mh, w), F32),
            out_p2=v((2, self.mh, w), F32),
            in_p2=v((2, self.mh, w), F32),
            pfull=v((tests, self.k), BF16),
            msend=v((self.each, W, W), BF16),
            mrecv=v((self.half, w, W), BF16),
            xsend=v((w, w), BF16),
            xrecv=v((w, w), BF16),
            dsend=v((w, self.each * W), BF16),
            drecv=v((w, self.each * W), BF16),
            ssem=pltpu.SemaphoreType.DMA((self.slots(),)),
            rsem=pltpu.SemaphoreType.DMA((self.slots(),)),
            msem=pltpu.SemaphoreType.DMA((2 * self.each,)),
            mrsem=pltpu.SemaphoreType.DMA((self.half,)),
            lsem=pltpu.SemaphoreType.DMA((4,)),
        )

    def slots(self):
        return 4 + 2 * self.far + 2 * self.far + 8 * self.far + 2 * self.far + 6 + 6 * self.far + 2 + 32


def kernel(s, names, g_hbm, t_hbm, f_hbm, term_ref, scores_ref, *refs):
    r = dict(zip(names, refs))
    n, far, w, W, chips, half, each = s.n, s.far, s.w, s.W, s.chips, s.half, s.each
    rows, mh, ra, rb = s.rows, s.mh, s.ra, s.rb
    me = lax.axis_index("dp")
    core, x, y, z = me % 2, me // 2 % 2, me // 4 % 2, me // 8
    q = me // 2

    def device(zz, yy, xx, cc):
        return ((zz * 2 + yy) * 2 + xx) * 2 + cc

    def up(g):
        return (z + g) % far

    def down(g):
        return (z + far - g) % far

    mate = device(z, y, x, 1 - core)
    x_to = device(z, y, 1 - x, core)
    y_to = device(z, 1 - y, x, core)
    ssem, rsem = r["ssem"], r["rsem"]
    started = []
    count = [0]

    def to(src, dst, target):
        i = count[0]
        count[0] += 1
        copy = pltpu.make_async_remote_copy(
            src_ref=src, dst_ref=dst, send_sem=ssem.at[i], recv_sem=rsem.at[i],
            device_id={"dp": target}, device_id_type=MESH,
        )
        copy.start()
        started.append(copy)
        return copy

    def lanes(block, width):
        return pl.ds(pl.multiple_of(block * width, width), width)

    barrier = pltpu.get_barrier_semaphore()

    def greet(i, carry):
        pl.semaphore_signal(barrier, inc=1, device_id={"dp": (me + i) % n}, device_id_type=MESH)
        return carry

    lax.fori_loop(1, n, greet, 0)
    pl.semaphore_wait(barrier, n - 1)

    gbuf, fbuf, tbuf = r["gbuf"], r["fbuf"], r["tbuf"]
    quarter = rows // 4
    g_copies = [
        to(g_hbm.at[pl.ds(i * quarter, quarter)], gbuf.at[pl.ds(rows + i * quarter, quarter)], mate)
        for i in range(4)
    ]
    g_own = pltpu.make_async_copy(g_hbm, gbuf.at[pl.ds(0, rows)], r["lsem"].at[0])
    g_own.start()
    t_own = pltpu.make_async_copy(t_hbm, tbuf.at[:, pl.ds(0, w)], r["lsem"].at[1])
    t_own.start()
    f_own = pltpu.make_async_copy(
        f_hbm.at[:, lanes(core * far + z, 4 * w)], fbuf.at[pl.ds(0, w)], r["lsem"].at[2]
    )
    f_own.start()
    t_copies = [
        to(t_hbm, tbuf.at[:, pl.ds(2 * g * w, w)], device(up(g), y, x, core)) for g in range(1, far)
    ]
    f_copies = [
        to(
            f_hbm.at[:, lanes((core + h) % 2 * far + up(g), 4 * w)],
            fbuf.at[pl.ds((2 * g + h) * w, w)],
            device(up(g), y, x, (core + h) % 2),
        )
        for g in range(far)
        for h in range(2)
        if g or h
    ]

    gt, tmp = r["gt"], r["tmp"]
    part_a, part_b, out_a1, out_b1 = r["part_a"], r["part_b"], r["out_a1"], r["out_b1"]

    def compute(g):
        def strip(u, carry):
            oy, ox = u // 2, u % 2
            own = (up(g) * 2 + (y + oy) % 2) * 2 + (x + ox) % 2
            gt[...] = gbuf[:, lanes(own, W)].T
            for e in range(each):
                col = (own + core * each + e) % chips
                tmp[e * W : (e + 1) * W] = jnp.dot(
                    gt[...], gbuf[:, lanes(col, W)], preferred_element_type=F32
                )
            col = 2 * ((own + half) % chips) + (core + own // half) % 2
            extra = jnp.dot(
                gt[pl.ds(pl.multiple_of(core * w, w), w), :], gbuf[:, lanes(col, w)],
                preferred_element_type=F32,
            )
            tmp[each * W :, :w] = extra[: w // 2]
            tmp[each * W :, w:] = extra[w // 2 :]

            @pl.when(ox == 0)
            def _():
                part_a[g, oy] = tmp[:ra]

            @pl.when(ox == 1)
            def _():
                out_a1[g, oy] = tmp[:ra].astype(BF16)

            @pl.when(oy == 0)
            def _():
                part_b[g, ox] = tmp[ra:]

            @pl.when(oy == 1)
            def _():
                out_b1[g, ox] = tmp[ra:].astype(BF16)

            return carry

        lax.fori_loop(0, 4, strip, 0)

    a1, b1, a2, b2, az, bz = {}, {}, {}, {}, {}, {}

    def first(g, o):
        a1[g, o] = to(out_a1.at[g, o], r["in_a1"].at[g, o], x_to)
        b1[g, o] = to(out_b1.at[g, o], r["in_b1"].at[g, o], y_to)

    def second(g):
        a1[g, 1].wait_recv()
        r["out_a2"][g] = (part_a[g, 1] + r["in_a1"][g, 1].astype(F32)).astype(BF16)
        a2[g] = to(r["out_a2"].at[g], r["in_a2"].at[g], y_to)
        b1[g, 1].wait_recv()
        r["out_b2"][g] = (part_b[g, 1] + r["in_b1"][g, 1].astype(F32)).astype(BF16)
        b2[g] = to(r["out_b2"].at[g], r["in_b2"].at[g], x_to)

    def third(g):
        a1[g, 0].wait_recv()
        a2[g].wait_recv()
        total = part_a[g, 0] + r["in_a1"][g, 0].astype(F32) + r["in_a2"][g].astype(F32)
        if g:
            r["out_az"][g - 1] = total.astype(BF16)
            az[g] = to(r["out_az"].at[g - 1], r["in_az"].at[g - 1], device(up(g), y, x, core))
        else:
            part_a[0, 0] = total
        b1[g, 0].wait_recv()
        b2[g].wait_recv()
        total = part_b[g, 0] + r["in_b1"][g, 0].astype(F32) + r["in_b2"][g].astype(F32)
        if g:
            r["out_bz"][g - 1] = total.astype(BF16)
            bz[g] = to(r["out_bz"].at[g - 1], r["in_bz"].at[g - 1], device(up(g), y, x, core))
        else:
            part_b[0, 0] = total

    pp, in_p1, out_p2, in_p2, pfull = r["pp"], r["in_p1"], r["out_p2"], r["in_p2"], r["pfull"]
    sub = lambda oy, ox: (y + oy) % 2 * 2 + (x + ox) % 2
    p1, p2 = {}, {}

    def hand_tests():
        t_own.wait()
        for copy in t_copies:
            copy.wait_recv()
        return [
            to(
                tbuf.at[:, pl.ds(2 * g * w, w)], tbuf.at[:, pl.ds((2 * g + 1) * w, w)], mate
            )
            for g in range(far)
        ]

    def precondition(handed):
        f_own.wait()
        for copy in f_copies + handed:
            copy.wait_recv()
        pp[...] = jnp.dot(tbuf[...], fbuf[...], preferred_element_type=F32)
        for o in (1, 0):
            p1[0, o] = to(pp.at[pl.ds(0, mh), lanes(sub(o, 1), w)], in_p1.at[0, o], x_to)
            p1[1, o] = to(pp.at[pl.ds(mh, mh), lanes(sub(1, o), w)], in_p1.at[1, o], y_to)

    def precondition_second():
        p1[0, 1].wait_recv()
        out_p2[0] = pp[:mh, lanes(sub(1, 0), w)] + in_p1[0, 1]
        p2[0] = to(out_p2.at[0], in_p2.at[0], y_to)
        p1[1, 1].wait_recv()
        out_p2[1] = pp[mh:, lanes(sub(0, 1), w)] + in_p1[1, 1]
        p2[1] = to(out_p2.at[1], in_p2.at[1], x_to)

    def place(zz, oy, ox):
        return lanes((core * far + zz) * 4 + sub(oy, ox), w)

    def pass_on(where, target):
        return to(pfull.at[:, where], pfull.at[:, where], target)

    def gather_first():
        p1[0, 0].wait_recv()
        p2[0].wait_recv()
        own = place(z, 0, 0)
        pfull[:mh, own] = (pp[:mh, lanes(sub(0, 0), w)] + in_p1[0, 0] + in_p2[0]).astype(BF16)
        p1[1, 0].wait_recv()
        p2[1].wait_recv()
        pfull[mh:, own] = (pp[mh:, lanes(sub(0, 0), w)] + in_p1[1, 0] + in_p2[1]).astype(BF16)
        return [pass_on(own, device(up(g), y, x, core)) for g in range(1, far)]

    def gather_second(along_z):
        for copy in along_z:
            copy.wait_recv()
        gx, gy = [], []
        for g in range(far):
            gx.append(pass_on(place(down(g), 0, 0), x_to))
            gy.append(pass_on(place(down(g), 0, 0), y_to))
        return gx, gy

    def gather_third(gx, gy):
        diagonal = []
        for g in range(far):
            gx[g].wait_recv()
            gy[g].wait_recv()
            if g % 2:
                diagonal.append(pass_on(place(down(g), 0, 1), y_to))
            else:
                diagonal.append(pass_on(place(down(g), 1, 0), x_to))
        return diagonal

    def gather_fourth(diagonal):
        mates = []
        for g in range(far):
            diagonal[g].wait_recv()
            where = lanes(core * far + down(g), 4 * w)
            mates.append(pass_on(where, mate))
        return mates

    def score(mates):
        for copy in mates:
            copy.wait_recv()
        scores_ref[...] = jnp.zeros_like(scores_ref)

        def chunk(i, carry):
            where = lanes(i, 4 * w)
            scores_ref[...] += lax.dot_general(
                gbuf[:rows, where], pfull[:, where], (((1,), (1,)), ((), ())),
                preferred_element_type=F32,
            )
            return carry

        lax.fori_loop(0, s.k // (4 * w), chunk, 0)

    msend, mrecv, msem, mrsem = r["msend"], r["mrecv"], r["msem"], r["mrsem"]
    dsend, drecv, xsend, xrecv = r["dsend"], r["drecv"], r["xsend"], r["xrecv"]

    def mirror_copy(e, side):
        d = core * each + e
        return pltpu.make_async_remote_copy(
            src_ref=msend.at[e, pl.ds(side * w, w)], dst_ref=mrecv.at[d],
            send_sem=msem.at[2 * e + side], recv_sem=mrsem.at[d],
            device_id={"dp": 2 * ((q + d) % chips) + side}, device_id_type=MESH,
        )

    def when_sent(e, act):
        if e:
            act()
        else:
            pl.when(core == 1)(act)

    def finish():
        for g in range(1, far):
            az[g].wait_recv()
            bz[g].wait_recv()
        for e in range(each):
            at = e * W
            part, came = (part_a, r["in_az"]) if at < ra else (part_b, r["in_bz"])
            at = at if at < ra else at - ra
            total = part[0, 0, at : at + W]
            for g in range(far - 1):
                total = total + came[g, at : at + W].astype(F32)
            tmp[e * W : (e + 1) * W] = total
            msend[e] = total.T.astype(BF16)

            def send(e=e):
                for side in range(2):
                    mirror_copy(e, side).start()

            when_sent(e, send)
            where = lanes((q + core * each + e) % chips, W)
            term_ref[:, where] = tmp[pl.ds(pl.multiple_of(e * W + core * w, w), w), :]
            other = pl.ds(pl.multiple_of(e * W + (1 - core) * w, w), w)
            dsend[:, e * W : (e + 1) * W] = tmp[other, :].astype(BF16)
        direct = to(dsend, drecv, mate)
        at = rb - w // 2
        total = part_b[0, 0, at:]
        for g in range(far - 1):
            total = total + r["in_bz"][g, at:].astype(F32)
        extra = jnp.concatenate([total[:, :w], total[:, w:]], axis=0)
        col = 2 * ((q + half) % chips) + (core + q // half) % 2
        term_ref[:, lanes(col, w)] = extra
        xsend[...] = extra.T.astype(BF16)
        mirrored = to(xsend, xrecv, col)
        return direct, mirrored

    def close(direct, mirrored):
        direct.wait_recv()
        for e in range(each):
            where = lanes((q + (1 - core) * each + e) % chips, W)
            term_ref[:, where] = drecv[:, e * W : (e + 1) * W].astype(F32)
        for d in range(1, half):
            pltpu.make_async_remote_copy(
                src_ref=mrecv.at[d], dst_ref=mrecv.at[d], send_sem=msem.at[0], recv_sem=mrsem.at[d],
                device_id={"dp": mate}, device_id_type=MESH,
            ).wait_recv()
            term_ref[:, lanes((q + chips - d) % chips, W)] = mrecv[d].astype(F32)
        mirrored.wait_recv()
        far_chip = (q + half) % chips
        col = 2 * far_chip + (core + far_chip // half) % 2
        term_ref[:, lanes(col, w)] = xrecv[...].astype(F32)

    order = list(range(1, far)) + [0]
    g_own.wait()
    for copy in g_copies:
        copy.wait_recv()
    compute(1)
    first(1, 1)
    first(1, 0)
    compute(2)
    first(2, 1)
    second(1)
    first(2, 0)
    handed = hand_tests()
    compute(3)
    first(3, 1)
    precondition(handed)
    third(1)
    second(2)
    first(3, 0)
    precondition_second()
    compute(0)
    first(0, 1)
    third(2)
    along_z = gather_first()
    second(3)
    first(0, 0)
    gx, gy = gather_second(along_z)
    third(3)
    second(0)
    diagonal = gather_third(gx, gy)
    third(0)
    direct, mirrored = finish()
    mates = gather_fourth(diagonal)
    score(mates)
    close(direct, mirrored)
    for copy in started:
        copy.wait_send()
    for e in range(each):

        def sent(e=e):
            for side in range(2):
                mirror_copy(e, side).wait_send()

        when_sent(e, sent)


def window(grads, covariance, test_grads, inverse_factor):
    n = lax.axis_size("dp")
    rows, k = grads.shape
    s = Sizes(n, rows, k, test_grads.shape[0])
    scratch = s.scratch()
    term, scores = pl.pallas_call(
        functools.partial(kernel, s, list(scratch)),
        out_shape=(
            jax.ShapeDtypeStruct((s.w, k), F32),
            jax.ShapeDtypeStruct((rows, s.tests), F32),
        ),
        in_specs=[pl.BlockSpec(memory_space=pl.ANY)] * 3,
        out_specs=(
            pl.BlockSpec(memory_space=pltpu.VMEM),
            pl.BlockSpec(memory_space=pltpu.VMEM),
        ),
        scratch_shapes=list(scratch.values()),
        compiler_params=pltpu.CompilerParams(
            collective_id=0, has_side_effects=True, vmem_limit_bytes=62 * 1024 * 1024
        ),
    )(grads, test_grads, inverse_factor)
    return scores, 0.9 * covariance + term / (rows * n)


def solution(mesh):
    placed = (P("dp", "feat"), P("dp", "feat"), P("feat", "dp"), P("dp", None))
    whole = mesh.shape["feat"] == 1 and mesh.shape["dp"] == 32
    return jax.shard_map(
        window if whole else general,
        mesh=mesh,
        in_specs=placed,
        out_specs=(P("dp", "feat"), P("dp", "feat")),
        check_vma=False,
    )
```

profile of v0, /device:TPU:0, one launch (start us, length us, event | category | flops | bytes accessed | tf_op | source)
XLA Modules:
  0.0 146.4 jit_solution(5458878633974834262)
XLA Ops:
  0.6 140.8 %shard_map.59 = (f32[128,4096]{1,0:T(8,128)}, f32[512,512]{1,0:T(8,128)}) custom-call(bf16[512,4096]{1,0:T(8,128)(2,1)} %g_hbm.1, bf16[512,128]{1,0:T(8,128)(2,1)} %t_hbm.1, bf16[128,4096]{1,0:T(8,128)(2,1)} %f_hbm.1), custom_call_target="tpu_custom_call" | custom-call | tf_op jit(solution)/shard_map/pallas_call | solution.py:448
  141.5 0.0 copy-start
  141.5 3.9 %multiply_add_fusion = f32[128,4096]{1,0:T(8,128)} fusion(f32[128,4096]{1,0:T(8,128)} %get-tuple-element.5, f32[128,4096]{1,0:T(8,128)} %param.5), kind=kLoop, calls=%fused_computation | loop fusion | flops 1572864 | bytes 6291456 | tf_op jit(solution)/shard_map/add | solution.py:464
  145.4 0.0 copy-done
  145.4 1.0 copy.7
Async XLA Ops:
  141.5 4.0 %copy-start = (f32[512,512]{1,0:T(8,128)S(1)}, f32[512,512]{1,0:T(8,128)}, u32[]{:S(2)}) copy-start(f32[512,512]{1,0:T(8,128)} %get-tuple-element.8) | copy-start | bytes 3145732
where the time goes:
time: 149 us; the launch traced here: 146 us
  Pallas kernels  141 us (95%)
  other arithmetic  3.94 us (3%)
    pallas_call x1, Pallas kernels, window(): pl.pallas_call(functools.partial(kernel, s, list(scratch)), out_shape=(ja...  141 us
    add x1, other arithmetic, window(): return (scores, 0.9 * covariance + term / (rows * n))  3.94 us

commit v1 on v0

--- a/solution.py
+++ b/solution.py
@@ -99,11 +99,8 @@
     def device(zz, yy, xx, cc):
         return ((zz * 2 + yy) * 2 + xx) * 2 + cc
 
-    def up(g):
-        return (z + g) % far
-
-    def down(g):
-        return (z + far - g) % far
+    def over(g):
+        return (z, z + 1 - 2 * (z % 2), (z + 2) % far, far - 1 - z)[g]
 
     mate = device(z, y, x, 1 - core)
     x_to = device(z, y, 1 - x, core)
@@ -126,50 +123,77 @@
     def lanes(block, width):
         return pl.ds(pl.multiple_of(block * width, width), width)
 
-    barrier = pltpu.get_barrier_semaphore()
-
-    def greet(i, carry):
-        pl.semaphore_signal(barrier, inc=1, device_id={"dp": (me + i) % n}, device_id_type=MESH)
-        return carry
-
-    lax.fori_loop(1, n, greet, 0)
-    pl.semaphore_wait(barrier, n - 1)
-
     gbuf, fbuf, tbuf = r["gbuf"], r["fbuf"], r["tbuf"]
-    quarter = rows // 4
-    g_copies = [
-        to(g_hbm.at[pl.ds(i * quarter, quarter)], gbuf.at[pl.ds(rows + i * quarter, quarter)], mate)
-        for i in range(4)
+    quarter = s.k // far
+    own_copies = [
+        pltpu.make_async_copy(g_hbm, gbuf.at[pl.ds(0, rows)], r["lsem"].at[0]),
+        pltpu.make_async_copy(t_hbm, tbuf.at[:, pl.ds(0, w)], r["lsem"].at[1]),
+        pltpu.make_async_copy(
+            f_hbm.at[:, lanes(core * far + z, 4 * w)], fbuf.at[pl.ds(0, w)], r["lsem"].at[2]
+        ),
     ]
-    g_own = pltpu.make_async_copy(g_hbm, gbuf.at[pl.ds(0, rows)], r["lsem"].at[0])
-    g_own.start()
-    t_own = pltpu.make_async_copy(t_hbm, tbuf.at[:, pl.ds(0, w)], r["lsem"].at[1])
-    t_own.start()
-    f_own = pltpu.make_async_copy(
-        f_hbm.at[:, lanes(core * far + z, 4 * w)], fbuf.at[pl.ds(0, w)], r["lsem"].at[2]
-    )
-    f_own.start()
-    t_copies = [
-        to(t_hbm, tbuf.at[:, pl.ds(2 * g * w, w)], device(up(g), y, x, core)) for g in range(1, far)
-    ]
-    f_copies = [
-        to(
-            f_hbm.at[:, lanes((core + h) % 2 * far + up(g), 4 * w)],
-            fbuf.at[pl.ds((2 * g + h) * w, w)],
-            device(up(g), y, x, (core + h) % 2),
-        )
-        for g in range(far)
-        for h in range(2)
-        if g or h
-    ]
+
+    def meet():
+        barrier = pltpu.get_barrier_semaphore()
+
+        for target in [mate, x_to, y_to] + [
+            device(over(g), y, x, (core + h) % 2) for g in range(1, far) for h in range(2)
+        ]:
+            pl.semaphore_signal(barrier, inc=1, device_id={"dp": target}, device_id_type=MESH)
+        for copy in own_copies:
+            copy.start()
+        pl.semaphore_wait(barrier, 2 * far + 1)
+
+    def swap_grads():
+        parts = [lanes((over(3) + i) % far, quarter) for i in range(far)]
+        return [
+            to(g_hbm.at[:, part], gbuf.at[pl.ds(rows, rows), part], mate) for part in parts
+        ]
+
+    def hand(g, target, came):
+        return to(tbuf.at[:, pl.ds(2 * g * w, w)], tbuf.at[:, pl.ds(came * w, w)], target)
+
+    def swap_tests():
+        return [
+            to(t_hbm, tbuf.at[:, pl.ds(2 * g * w, w)], device(over(g), y, x, core)) for g in (1, 2)
+        ]
+
+    def swap_factor(*groups):
+        return [
+            to(
+                f_hbm.at[:, lanes((core + h) % 2 * far + over(g), 4 * w)],
+                fbuf.at[pl.ds((2 * g + h) * w, w)],
+                device(over(g), y, x, (core + h) % 2),
+            )
+            for g in groups
+            for h in range(2)
+            if g or h
+        ]
+
+    def relay_tests(copies):
+        copies[1].wait_recv()
+        return hand(2, device(over(1), y, x, core), 6)
+
+    def hand_tests(copies):
+        own_copies[1].wait()
+        copies[0].wait_recv()
+        return [hand(g, mate, 2 * g + 1) for g in range(3)]
+
+    def hand_relayed(copy):
+        copy.wait_recv()
+        return [hand(3, mate, 7)]
+
+    def grads_here(copies):
+        for copy in copies:
+            copy.wait_recv()
 
     gt, tmp = r["gt"], r["tmp"]
     part_a, part_b, out_a1, out_b1 = r["part_a"], r["part_b"], r["out_a1"], r["out_b1"]
 
-    def compute(g):
-        def strip(u, carry):
-            oy, ox = u // 2, u % 2
-            own = (up(g) * 2 + (y + oy) % 2) * 2 + (x + ox) % 2
+    def compute(g, first=0, last=4):
+        def strip(i, carry):
+            oy, ox = (3 - i) // 2, (3 - i) % 2
+            own = (over(g) * 2 + (y + oy) % 2) * 2 + (x + ox) % 2
             gt[...] = gbuf[:, lanes(own, W)].T
             for e in range(each):
                 col = (own + core * each + e) % chips
@@ -202,7 +226,7 @@
 
             return carry
 
-        lax.fori_loop(0, 4, strip, 0)
+        lax.fori_loop(first, last, strip, 0)
 
     a1, b1, a2, b2, az, bz = {}, {}, {}, {}, {}, {}
 
@@ -221,39 +245,33 @@
     def third(g):
         a1[g, 0].wait_recv()
         a2[g].wait_recv()
-        total = part_a[g, 0] + r["in_a1"][g, 0].astype(F32) + r["in_a2"][g].astype(F32)
-        if g:
-            r["out_az"][g - 1] = total.astype(BF16)
-            az[g] = to(r["out_az"].at[g - 1], r["in_az"].at[g - 1], device(up(g), y, x, core))
-        else:
-            part_a[0, 0] = total
+        total_a = part_a[g, 0] + r["in_a1"][g, 0].astype(F32) + r["in_a2"][g].astype(F32)
         b1[g, 0].wait_recv()
         b2[g].wait_recv()
-        total = part_b[g, 0] + r["in_b1"][g, 0].astype(F32) + r["in_b2"][g].astype(F32)
-        if g:
-            r["out_bz"][g - 1] = total.astype(BF16)
-            bz[g] = to(r["out_bz"].at[g - 1], r["in_bz"].at[g - 1], device(up(g), y, x, core))
-        else:
-            part_b[0, 0] = total
+        total_b = part_b[g, 0] + r["in_b1"][g, 0].astype(F32) + r["in_b2"][g].astype(F32)
+        if g == 0:
+            part_a[0, 0] = total_a
+            part_b[0, 0] = total_b
+            return
+        if g == 2:
+            az[3].wait_recv()
+            total_a = total_a + r["in_az"][2].astype(F32)
+            bz[3].wait_recv()
+            total_b = total_b + r["in_bz"][2].astype(F32)
+        target = device(over(2 if g == 2 else 1), y, x, core)
+        slot = {3: 2, 2: 1, 1: 0}[g]
+        r["out_az"][slot] = total_a.astype(BF16)
+        az[g] = to(r["out_az"].at[slot], r["in_az"].at[slot], target)
+        r["out_bz"][slot] = total_b.astype(BF16)
+        bz[g] = to(r["out_bz"].at[slot], r["in_bz"].at[slot], target)
 
     pp, in_p1, out_p2, in_p2, pfull = r["pp"], r["in_p1"], r["out_p2"], r["in_p2"], r["pfull"]
     sub = lambda oy, ox: (y + oy) % 2 * 2 + (x + ox) % 2
     p1, p2 = {}, {}
 
-    def hand_tests():
-        t_own.wait()
-        for copy in t_copies:
-            copy.wait_recv()
-        return [
-            to(
-                tbuf.at[:, pl.ds(2 * g * w, w)], tbuf.at[:, pl.ds((2 * g + 1) * w, w)], mate
-            )
-            for g in range(far)
-        ]
-
     def precondition(handed):
-        f_own.wait()
-        for copy in f_copies + handed:
+        own_copies[2].wait()
+        for copy in handed:
             copy.wait_recv()
         pp[...] = jnp.dot(tbuf[...], fbuf[...], preferred_element_type=F32)
         for o in (1, 0):
@@ -268,8 +286,8 @@
         out_p2[1] = pp[mh:, lanes(sub(0, 1), w)] + in_p1[1, 1]
         p2[1] = to(out_p2.at[1], in_p2.at[1], x_to)
 
-    def place(zz, oy, ox):
-        return lanes((core * far + zz) * 4 + sub(oy, ox), w)
+    def place(oy, ox, part=0, parts=1):
+        return lanes((core * 4 + sub(oy, ox)) * parts + part, far * w // parts)
 
     def pass_on(where, target):
         return to(pfull.at[:, where], pfull.at[:, where], target)
@@ -277,55 +295,54 @@
     def gather_first():
         p1[0, 0].wait_recv()
         p2[0].wait_recv()
-        own = place(z, 0, 0)
+        own = lanes((core * 4 + sub(0, 0)) * far + z, w)
         pfull[:mh, own] = (pp[:mh, lanes(sub(0, 0), w)] + in_p1[0, 0] + in_p2[0]).astype(BF16)
         p1[1, 0].wait_recv()
         p2[1].wait_recv()
         pfull[mh:, own] = (pp[mh:, lanes(sub(0, 0), w)] + in_p1[1, 0] + in_p2[1]).astype(BF16)
-        return [pass_on(own, device(up(g), y, x, core)) for g in range(1, far)]
-
-    def gather_second(along_z):
-        for copy in along_z:
+        return [pass_on(own, device(over(g), y, x, core)) for g in (1, 2)]
+
+    def gather_relay(along_z):
+        along_z[1].wait_recv()
+        there = lanes((core * 4 + sub(0, 0)) * far + over(2), w)
+        return pass_on(there, device(over(1), y, x, core))
+
+    def gather_second(along_z, relayed):
+        along_z[0].wait_recv()
+        relayed.wait_recv()
+        own = place(0, 0)
+        return pass_on(own, x_to), pass_on(own, y_to), pass_on(own, mate)
+
+    def gather_third(gx, gy):
+        gx.wait_recv()
+        diagonal = [pass_on(place(0, 1, 0, 2), y_to)]
+        mates = [pass_on(place(0, 1), mate)]
+        gy.wait_recv()
+        diagonal.append(pass_on(place(1, 0, 1, 2), x_to))
+        mates.append(pass_on(place(1, 0), mate))
+        return diagonal, mates
+
+    def gather_fourth(diagonal):
+        for copy in diagonal:
             copy.wait_recv()
-        gx, gy = [], []
-        for g in range(far):
-            gx.append(pass_on(place(down(g), 0, 0), x_to))
-            gy.append(pass_on(place(down(g), 0, 0), y_to))
-        return gx, gy
-
-    def gather_third(gx, gy):
-        diagonal = []
-        for g in range(far):
-            gx[g].wait_recv()
-            gy[g].wait_recv()
-            if g % 2:
-                diagonal.append(pass_on(place(down(g), 0, 1), y_to))
-            else:
-                diagonal.append(pass_on(place(down(g), 1, 0), x_to))
-        return diagonal
-
-    def gather_fourth(diagonal):
-        mates = []
-        for g in range(far):
-            diagonal[g].wait_recv()
-            where = lanes(core * far + down(g), 4 * w)
-            mates.append(pass_on(where, mate))
-        return mates
-
-    def score(mates):
-        for copy in mates:
-            copy.wait_recv()
-        scores_ref[...] = jnp.zeros_like(scores_ref)
-
+        return pass_on(place(1, 1), mate)
+
+    def score(other, first, last):
         def chunk(i, carry):
-            where = lanes(i, 4 * w)
+            cc, at = (core + other) % 2, sub(i // 2, i % 2)
+            left = jnp.concatenate(
+                [gbuf[:rows, lanes((cc * far + zz) * 4 + at, w)] for zz in range(far)], axis=1
+            )
             scores_ref[...] += lax.dot_general(
-                gbuf[:rows, where], pfull[:, where], (((1,), (1,)), ((), ())),
+                left, pfull[:, lanes(cc * 4 + at, far * w)], (((1,), (1,)), ((), ())),
                 preferred_element_type=F32,
             )
             return carry
 
-        lax.fori_loop(0, s.k // (4 * w), chunk, 0)
+        lax.fori_loop(first, last, chunk, 0)
+
+    def scores_start():
+        scores_ref[...] = jnp.zeros_like(scores_ref)
 
     msend, mrecv, msem, mrsem = r["msend"], r["mrecv"], r["msem"], r["mrsem"]
     dsend, drecv, xsend, xrecv = r["dsend"], r["drecv"], r["xsend"], r["xrecv"]
@@ -345,7 +362,7 @@
             pl.when(core == 1)(act)
 
     def finish():
-        for g in range(1, far):
+        for g in (1, 2):
             az[g].wait_recv()
             bz[g].wait_recv()
         for e in range(each):
@@ -353,7 +370,7 @@
             part, came = (part_a, r["in_az"]) if at < ra else (part_b, r["in_bz"])
             at = at if at < ra else at - ra
             total = part[0, 0, at : at + W]
-            for g in range(far - 1):
+            for g in range(2):
                 total = total + came[g, at : at + W].astype(F32)
             tmp[e * W : (e + 1) * W] = total
             msend[e] = total.T.astype(BF16)
@@ -370,7 +387,7 @@
         direct = to(dsend, drecv, mate)
         at = rb - w // 2
         total = part_b[0, 0, at:]
-        for g in range(far - 1):
+        for g in range(2):
             total = total + r["in_bz"][g, at:].astype(F32)
         extra = jnp.concatenate([total[:, :w], total[:, w:]], axis=0)
         col = 2 * ((q + half) % chips) + (core + q // half) % 2
@@ -395,50 +412,67 @@
         col = 2 * far_chip + (core + far_chip // half) % 2
         term_ref[:, lanes(col, w)] = xrecv[...].astype(F32)
 
-    order = list(range(1, far)) + [0]
-    g_own.wait()
-    for copy in g_copies:
-        copy.wait_recv()
-    compute(1)
-    first(1, 1)
-    first(1, 0)
+    def wait_sends():
+        for copy in started:
+            copy.wait_send()
+        for e in range(each):
+
+            def sent(e=e):
+                for side in range(2):
+                    mirror_copy(e, side).wait_send()
+
+            when_sent(e, sent)
+
+    meet()
+    swapped = swap_grads()
+    t_copies = swap_tests()
+    own_copies[0].wait()
+    grads_here(swapped[:3])
+    early = swap_factor(0, 3, 2, 1)
+    compute(3, 0, 1)
+    first(3, 1)
+    relayed = relay_tests(t_copies)
+    compute(3, 1, 3)
+    first(3, 0)
+    compute(3, 3, 4)
+    grads_here(swapped[3:])
     compute(2)
     first(2, 1)
+    early += hand_tests(t_copies)
+    second(3)
+    first(2, 0)
+    early += hand_relayed(relayed)
+    compute(1)
+    precondition(early)
+    first(1, 1)
+    third(3)
+    precondition_second()
+    second(2)
+    first(1, 0)
+    compute(0)
+    along_z = gather_first()
+    third(2)
+    first(0, 1)
+    relayed = gather_relay(along_z)
     second(1)
-    first(2, 0)
-    handed = hand_tests()
-    compute(3)
-    first(3, 1)
-    precondition(handed)
+    first(0, 0)
+    second(0)
+    gx, gy, mate_own = gather_second(along_z, relayed)
     third(1)
-    second(2)
-    first(3, 0)
-    precondition_second()
-    compute(0)
-    first(0, 1)
-    third(2)
-    along_z = gather_first()
-    second(3)
-    first(0, 0)
-    gx, gy = gather_second(along_z)
-    third(3)
-    second(0)
-    diagonal = gather_third(gx, gy)
+    scores_start()
+    score(0, 0, 1)
     third(0)
     direct, mirrored = finish()
-    mates = gather_fourth(diagonal)
-    score(mates)
+    diagonal, mates = gather_third(gx, gy)
+    score(0, 1, 3)
+    mate_diagonal = gather_fourth(diagonal)
+    grads_here([mate_own] + mates)
+    score(1, 0, 3)
+    score(0, 3, 4)
+    grads_here([mate_diagonal])
+    score(1, 3, 4)
     close(direct, mirrored)
-    for copy in started:
-        copy.wait_send()
-    for e in range(each):
-
-        def sent(e=e):
-            for side in range(2):
-                mirror_copy(e, side).wait_send()
-
-        when_sent(e, sent)
-
+    wait_sends()
 
 def window(grads, covariance, test_grads, inverse_factor):
     n = lax.axis_size("dp")
@@ -451,16 +485,16 @@
             jax.ShapeDtypeStruct((s.w, k), F32),
             jax.ShapeDtypeStruct((rows, s.tests), F32),
         ),
-        in_specs=[pl.BlockSpec(memory_space=pl.ANY)] * 3,
+        in_specs=[pl.BlockSpec(memory_space=pltpu.HBM)] * 3,
         out_specs=(
             pl.BlockSpec(memory_space=pltpu.VMEM),
             pl.BlockSpec(memory_space=pltpu.VMEM),
         ),
         scratch_shapes=list(scratch.values()),
         compiler_params=pltpu.CompilerParams(
-            collective_id=0, has_side_effects=True, vmem_limit_bytes=62 * 1024 * 1024
+            collective_id=0, has_side_effects=True, vmem_limit_bytes=49 * 1024 * 1024
         ),
-    )(grads, test_grads, inverse_factor)
+    )(*(pltpu.with_memory_space_constraint(a, pltpu.HBM) for a in (grads, test_grads, inverse_factor)))
     return scores, 0.9 * covariance + term / (rows * n)
 
 

time: 149 us -> 127 us (0.85); the launches traced: 146 us -> 126 us
  Pallas kernels: 141 us -> 123 us
  other arithmetic: 3.94 us -> 1.65 us
    pallas_call x1, Pallas kernels: 141 us -> 123 us  [window(): pl.pallas_call(functools.partial(kernel, s, list(scratch)), out_shape=(ja...]
    add x1, other arithmetic: 3.94 us -> 1.65 us  [window(): return (scores, 0.9 * covariance + term / (rows * n))]
where the time goes in v1:
time: 127 us; the launch traced here: 126 us
  Pallas kernels  123 us (97%)
  other arithmetic  1.65 us (1%)
    pallas_call x1, Pallas kernels, window(): pl.pallas_call(functools.partial(kernel, s, list(scratch)), out_shape=(ja...  123 us

profile of v1, /device:TPU:0, one launch (start us, length us, event | category | flops | bytes accessed | tf_op | source)
XLA Modules:
  0.0 126.4 jit_solution(14792113836557139568)
XLA Ops:
  0.6 0.0 copy-start
  0.6 123.2 %shard_map.59 = (f32[128,4096]{1,0:T(8,128)S(1)}, f32[512,512]{1,0:T(8,128)S(1)}) custom-call(bf16[512,4096]{1,0:T(8,128)(2,1)} %g_hbm.1, bf16[512,128]{1,0:T(8,128)(2,1)} %t_hbm.1, bf16[128,4096]{1,0:T(8,128)(2,1)} %f_hbm.1), custom_call_target="tpu_custom_call" | custom-call | tf_op jit(solution)/shard_map/pallas_call | solution.py:482
  123.8 0.0 copy-done
  123.8 1.6 %multiply_add_fusion = f32[128,4096]{1,0:T(8,128)} fusion(f32[128,4096]{1,0:T(8,128)S(1)} %get-tuple-element.5, f32[128,4096]{1,0:T(8,128)S(1)} %copy-done), kind=kLoop, calls=%fused_computation | loop fusion | flops 1572864 | bytes 6291456 | tf_op jit(solution)/shard_map/add | solution.py:498
  125.5 1.0 copy.7
Async XLA Ops:
  0.6 123.2 %copy-start = (f32[128,4096]{1,0:T(8,128)S(1)}, f32[128,4096]{1,0:T(8,128)}, u32[]{:S(2)}) copy-start(f32[128,4096]{1,0:T(8,128)} %param.5) | copy-start | bytes 6291460

commit v2 on v1

--- a/solution.py
+++ b/solution.py
@@ -85,7 +85,7 @@
         )
 
     def slots(self):
-        return 4 + 2 * self.far + 2 * self.far + 8 * self.far + 2 * self.far + 6 + 6 * self.far + 2 + 32
+        return 63 + self.chips + 2
 
 
 def kernel(s, names, g_hbm, t_hbm, f_hbm, term_ref, scores_ref, *refs):
@@ -124,7 +124,6 @@
         return pl.ds(pl.multiple_of(block * width, width), width)
 
     gbuf, fbuf, tbuf = r["gbuf"], r["fbuf"], r["tbuf"]
-    quarter = s.k // far
     own_copies = [
         pltpu.make_async_copy(g_hbm, gbuf.at[pl.ds(0, rows)], r["lsem"].at[0]),
         pltpu.make_async_copy(t_hbm, tbuf.at[:, pl.ds(0, w)], r["lsem"].at[1]),
@@ -145,7 +144,13 @@
         pl.semaphore_wait(barrier, 2 * far + 1)
 
     def swap_grads():
-        parts = [lanes((over(3) + i) % far, quarter) for i in range(far)]
+        there = 1 - core
+        begin = (over(3) * 2 + 1 - y) * 2 + 1 - x
+        last = half // 2
+        steps = [0] + [i + last * there for i in range(1, last)]
+        steps += [half - last * there, last + last * there]
+        steps += [i - last * there for i in range(last + 1, half)] + list(range(half + 1, chips))
+        parts = [lanes((begin + i) % chips, W) for i in steps]
         return [
             to(g_hbm.at[:, part], gbuf.at[pl.ds(rows, rows), part], mate) for part in parts
         ]
@@ -310,15 +315,18 @@
     def gather_second(along_z, relayed):
         along_z[0].wait_recv()
         relayed.wait_recv()
-        own = place(0, 0)
-        return pass_on(own, x_to), pass_on(own, y_to), pass_on(own, mate)
+        gx = [pass_on(place(0, 0, i, 2), x_to) for i in range(2)]
+        gy = [pass_on(place(0, 0, i, 2), y_to) for i in (1, 0)]
+        return gx, gy, pass_on(place(0, 0), mate)
 
     def gather_third(gx, gy):
-        gx.wait_recv()
+        gx[0].wait_recv()
         diagonal = [pass_on(place(0, 1, 0, 2), y_to)]
+        gy[0].wait_recv()
+        diagonal.append(pass_on(place(1, 0, 1, 2), x_to))
+        gx[1].wait_recv()
         mates = [pass_on(place(0, 1), mate)]
-        gy.wait_recv()
-        diagonal.append(pass_on(place(1, 0, 1, 2), x_to))
+        gy[1].wait_recv()
         mates.append(pass_on(place(1, 0), mate))
         return diagonal, mates
 
@@ -413,6 +421,7 @@
         term_ref[:, lanes(col, w)] = xrecv[...].astype(F32)
 
     def wait_sends():
+        assert count[0] == s.slots()
         for copy in started:
             copy.wait_send()
         for e in range(each):
@@ -427,15 +436,15 @@
     swapped = swap_grads()
     t_copies = swap_tests()
     own_copies[0].wait()
-    grads_here(swapped[:3])
+    grads_here(swapped[: half // 2 + 2])
     early = swap_factor(0, 3, 2, 1)
     compute(3, 0, 1)
     first(3, 1)
     relayed = relay_tests(t_copies)
+    grads_here(swapped[half // 2 + 2 :])
     compute(3, 1, 3)
     first(3, 0)
     compute(3, 3, 4)
-    grads_here(swapped[3:])
     compute(2)
     first(2, 1)
     early += hand_tests(t_copies)
@@ -465,9 +474,9 @@
     direct, mirrored = finish()
     diagonal, mates = gather_third(gx, gy)
     score(0, 1, 3)
-    mate_diagonal = gather_fourth(diagonal)
     grads_here([mate_own] + mates)
     score(1, 0, 3)
+    mate_diagonal = gather_fourth(diagonal)
     score(0, 3, 4)
     grads_here([mate_diagonal])
     score(1, 3, 4)

time: 127 us -> 123 us (0.969)
  Pallas kernels: 123 us -> 119 us
    pallas_call x1, Pallas kernels: 123 us -> 119 us  [window(): pl.pallas_call(functools.partial(kernel, s, list(scratch)), out_shape=(ja...]
where the time goes in v2:
time: 123 us
  Pallas kernels  119 us (97%)
  other arithmetic  1.65 us (1%)
    pallas_call x1, Pallas kernels, window(): pl.pallas_call(functools.partial(kernel, s, list(scratch)), out_shape=(ja...  119 us

profile of v2, /device:TPU:0, one launch (start us, length us, event | category | flops | bytes accessed | tf_op | source)
XLA Modules:
  0.0 122.7 jit_solution(6726472144838078626)
XLA Ops:
  0.6 0.0 copy-start
  0.6 119.4 %shard_map.59 = (f32[128,4096]{1,0:T(8,128)S(1)}, f32[512,512]{1,0:T(8,128)S(1)}) custom-call(bf16[512,4096]{1,0:T(8,128)(2,1)} %g_hbm.1, bf16[512,128]{1,0:T(8,128)(2,1)} %t_hbm.1, bf16[128,4096]{1,0:T(8,128)(2,1)} %f_hbm.1), custom_call_target="tpu_custom_call" | custom-call | tf_op jit(solution)/shard_map/pallas_call | solution.py:491
  120.1 0.0 copy-done
  120.1 1.6 %multiply_add_fusion = f32[128,4096]{1,0:T(8,128)} fusion(f32[128,4096]{1,0:T(8,128)S(1)} %get-tuple-element.5, f32[128,4096]{1,0:T(8,128)S(1)} %copy-done), kind=kLoop, calls=%fused_computation | loop fusion | flops 1572864 | bytes 6291456 | tf_op jit(solution)/shard_map/add | solution.py:507
  121.7 1.0 copy.7
Async XLA Ops:
  0.6 119.4 %copy-start = (f32[128,4096]{1,0:T(8,128)S(1)}, f32[128,4096]{1,0:T(8,128)}, u32[]{:S(2)}) copy-start(f32[128,4096]{1,0:T(8,128)} %param.5) | copy-start | bytes 6291460

commit v3 on v2

--- a/solution.py
+++ b/solution.py
@@ -38,8 +38,10 @@
         self.W = 2 * self.w
         self.half = self.chips // 2
         self.each = self.half // 2
-        self.ra = self.each // 2 * self.W
-        self.rb = (self.each - self.each // 2) * self.W + self.w // 2
+        self.strip = self.each * self.W + self.w // 2
+        self.rc = self.w // 2
+        self.ra = (self.strip - self.rc) // 2
+        self.rb = self.ra
         self.mh = tests // 2
 
     def scratch(self):
@@ -49,7 +51,7 @@
         return dict(
             gbuf=v((2 * self.rows, self.k), BF16),
             gt=v((W, 2 * self.rows), BF16),
-            tmp=v((self.ra + self.rb, W), F32),
+            tmp=v((self.strip, W), F32),
             part_a=v((far, 2, self.ra, W), F32),
             part_b=v((far, 2, self.rb, W), F32),
             out_a1=v((far, 2, self.ra, W), BF16),
@@ -64,6 +66,15 @@
             out_bz=v((far1, self.rb, W), BF16),
             in_az=v((far1, self.ra, W), BF16),
             in_bz=v((far1, self.rb, W), BF16),
+            part_c=v((2, 4, self.rc, W), F32),
+            out_c1=v((2, 4, self.rc, W), BF16),
+            in_c1=v((2, 4, self.rc, W), BF16),
+            out_c2=v((4, self.rc, W), BF16),
+            in_c2=v((4, self.rc, W), BF16),
+            out_c3=v((2, 2, self.rc // 2, W), BF16),
+            in_c3=v((2, 2, self.rc // 2, W), BF16),
+            out_c4=v((2, self.rc // 2, W), BF16),
+            in_c4=v((2, self.rc // 2, W), BF16),
             fbuf=v((2 * far * w, 4 * w), BF16),
             tbuf=v((tests, 2 * far * w), BF16),
             pp=v((tests, 4 * w), F32),
@@ -85,7 +96,7 @@
         )
 
     def slots(self):
-        return 63 + self.chips + 2
+        return 72 + self.chips
 
 
 def kernel(s, names, g_hbm, t_hbm, f_hbm, term_ref, scores_ref, *refs):
@@ -193,6 +204,10 @@
             copy.wait_recv()
 
     gt, tmp = r["gt"], r["tmp"]
+    part_c, out_c1, in_c1, out_c2, in_c2 = (
+        r["part_c"], r["out_c1"], r["in_c1"], r["out_c2"], r["in_c2"]
+    )
+    out_c3, in_c3, out_c4, in_c4 = r["out_c3"], r["in_c3"], r["out_c4"], r["in_c4"]
     part_a, part_b, out_a1, out_b1 = r["part_a"], r["part_b"], r["out_a1"], r["out_b1"]
 
     def compute(g, first=0, last=4):
@@ -223,12 +238,16 @@
 
             @pl.when(oy == 0)
             def _():
-                part_b[g, ox] = tmp[ra:]
+                part_b[g, ox] = tmp[ra : ra + rb]
 
             @pl.when(oy == 1)
             def _():
-                out_b1[g, ox] = tmp[ra:].astype(BF16)
-
+                out_b1[g, ox] = tmp[ra : ra + rb].astype(BF16)
+
+            if g % 2:
+                out_c1[g // 2, 3 - i] = tmp[ra + rb :].astype(BF16)
+            else:
+                part_c[g // 2, 3 - i] = tmp[ra + rb :]
             return carry
 
         lax.fori_loop(first, last, strip, 0)
@@ -270,6 +289,36 @@
         r["out_bz"][slot] = total_b.astype(BF16)
         bz[g] = to(r["out_bz"].at[slot], r["in_bz"].at[slot], target)
 
+    c1, c2, c3, c4 = {}, [], {}, {}
+    hc = s.rc // 2
+
+    def c_first():
+        for slot in (1, 0):
+            c1[slot] = to(out_c1.at[slot], in_c1.at[slot], device(over(1), y, x, core))
+
+    def c_second():
+        c1[1].wait_recv()
+        out_c2[...] = (part_c[1] + in_c1[1].astype(F32)).astype(BF16)
+        c2.append(to(out_c2, in_c2, device(over(2), y, x, core)))
+
+    def c_third():
+        c1[0].wait_recv()
+        c2[0].wait_recv()
+        part_c[0] = part_c[0] + in_c1[0].astype(F32) + in_c2[...].astype(F32)
+        for o in range(2):
+            out_c3[0, o] = part_c[0, 2 * o + 1, :hc].astype(BF16)
+            out_c3[1, o] = part_c[0, 2 + o, hc:].astype(BF16)
+        c3[0] = to(out_c3.at[0], in_c3.at[0], x_to)
+        c3[1] = to(out_c3.at[1], in_c3.at[1], y_to)
+
+    def c_fourth():
+        c3[0].wait_recv()
+        out_c4[0] = (part_c[0, 2, :hc] + in_c3[0, 1].astype(F32)).astype(BF16)
+        c4[0] = to(out_c4.at[0], in_c4.at[0], y_to)
+        c3[1].wait_recv()
+        out_c4[1] = (part_c[0, 1, hc:] + in_c3[1, 1].astype(F32)).astype(BF16)
+        c4[1] = to(out_c4.at[1], in_c4.at[1], x_to)
+
     pp, in_p1, out_p2, in_p2, pfull = r["pp"], r["in_p1"], r["out_p2"], r["in_p2"], r["pfull"]
     sub = lambda oy, ox: (y + oy) % 2 * 2 + (x + ox) % 2
     p1, p2 = {}, {}
@@ -323,12 +372,13 @@
         gx[0].wait_recv()
         diagonal = [pass_on(place(0, 1, 0, 2), y_to)]
         gy[0].wait_recv()
-        diagonal.append(pass_on(place(1, 0, 1, 2), x_to))
+        return diagonal + [pass_on(place(1, 0, 1, 2), x_to)]
+
+    def gather_mates(gx, gy):
         gx[1].wait_recv()
         mates = [pass_on(place(0, 1), mate)]
         gy[1].wait_recv()
-        mates.append(pass_on(place(1, 0), mate))
-        return diagonal, mates
+        return mates + [pass_on(place(1, 0), mate)]
 
     def gather_fourth(diagonal):
         for copy in diagonal:
@@ -369,19 +419,28 @@
         else:
             pl.when(core == 1)(act)
 
-    def finish():
-        for g in (1, 2):
-            az[g].wait_recv()
-            bz[g].wait_recv()
+    def finish(part):
+        if part < 2:
+            sums, came, copies, size = (
+                (part_a, r["in_az"], az, ra), (part_b, r["in_bz"], bz, rb)
+            )[part]
+            at = part * ra
+            for g in (1, 2):
+                copies[g].wait_recv()
+            tmp[at : at + size] = sums[0, 0] + came[0].astype(F32) + came[1].astype(F32)
+        else:
+            at, size = ra + rb, s.rc
+            for i in range(2):
+                c4[i].wait_recv()
+                tmp[at + i * hc : at + (i + 1) * hc] = (
+                    part_c[0, 0, i * hc : (i + 1) * hc]
+                    + in_c3[i, 0].astype(F32)
+                    + in_c4[i].astype(F32)
+                )
         for e in range(each):
-            at = e * W
-            part, came = (part_a, r["in_az"]) if at < ra else (part_b, r["in_bz"])
-            at = at if at < ra else at - ra
-            total = part[0, 0, at : at + W]
-            for g in range(2):
-                total = total + came[g, at : at + W].astype(F32)
-            tmp[e * W : (e + 1) * W] = total
-            msend[e] = total.T.astype(BF16)
+            if not at < (e + 1) * W <= at + size:
+                continue
+            msend[e] = tmp[e * W : (e + 1) * W].T.astype(BF16)
 
             def send(e=e):
                 for side in range(2):
@@ -392,12 +451,10 @@
             term_ref[:, where] = tmp[pl.ds(pl.multiple_of(e * W + core * w, w), w), :]
             other = pl.ds(pl.multiple_of(e * W + (1 - core) * w, w), w)
             dsend[:, e * W : (e + 1) * W] = tmp[other, :].astype(BF16)
+        if part < 2:
+            return None
         direct = to(dsend, drecv, mate)
-        at = rb - w // 2
-        total = part_b[0, 0, at:]
-        for g in range(2):
-            total = total + r["in_bz"][g, at:].astype(F32)
-        extra = jnp.concatenate([total[:, :w], total[:, w:]], axis=0)
+        extra = jnp.concatenate([tmp[each * W :, :w], tmp[each * W :, w:]], axis=0)
         col = 2 * ((q + half) % chips) + (core + q // half) % 2
         term_ref[:, lanes(col, w)] = extra
         xsend[...] = extra.T.astype(BF16)
@@ -452,27 +509,34 @@
     first(2, 0)
     early += hand_relayed(relayed)
     compute(1)
+    c_first()
+    third(3)
     precondition(early)
     first(1, 1)
-    third(3)
     precondition_second()
     second(2)
     first(1, 0)
     compute(0)
+    c_second()
     along_z = gather_first()
     third(2)
     first(0, 1)
+    second(1)
+    c_third()
+    first(0, 0)
     relayed = gather_relay(along_z)
-    second(1)
-    first(0, 0)
     second(0)
+    c_fourth()
     gx, gy, mate_own = gather_second(along_z, relayed)
     third(1)
     scores_start()
     score(0, 0, 1)
     third(0)
-    direct, mirrored = finish()
-    diagonal, mates = gather_third(gx, gy)
+    diagonal = gather_third(gx, gy)
+    finish(0)
+    finish(1)
+    direct, mirrored = finish(2)
+    mates = gather_mates(gx, gy)
     score(0, 1, 3)
     grads_here([mate_own] + mates)
     score(1, 0, 3)

time: 123 us -> 119 us (0.967)
  Pallas kernels: 119 us -> 115 us
    pallas_call x1, Pallas kernels: 119 us -> 115 us  [window(): pl.pallas_call(functools.partial(kernel, s, list(scratch)), out_shape=(ja...]
where the time goes in v3:
time: 119 us
  Pallas kernels  115 us (97%)
  other arithmetic  1.65 us (1%)
    pallas_call x1, Pallas kernels, window(): pl.pallas_call(functools.partial(kernel, s, list(scratch)), out_shape=(ja...  115 us

profile of v3, /device:TPU:0, one launch (start us, length us, event | category | flops | bytes accessed | tf_op | source)
XLA Modules:
  0.0 118.7 jit_solution(8437992592416214160)
XLA Ops:
  0.6 0.0 copy-start
  0.6 115.4 %shard_map.59 = (f32[128,4096]{1,0:T(8,128)S(1)}, f32[512,512]{1,0:T(8,128)S(1)}) custom-call(bf16[512,4096]{1,0:T(8,128)(2,1)} %g_hbm.1, bf16[512,128]{1,0:T(8,128)(2,1)} %t_hbm.1, bf16[128,4096]{1,0:T(8,128)(2,1)} %f_hbm.1), custom_call_target="tpu_custom_call" | custom-call | tf_op jit(solution)/shard_map/pallas_call | solution.py:555
  116.1 0.0 copy-done
  116.1 1.6 %multiply_add_fusion = f32[128,4096]{1,0:T(8,128)} fusion(f32[128,4096]{1,0:T(8,128)S(1)} %get-tuple-element.5, f32[128,4096]{1,0:T(8,128)S(1)} %copy-done), kind=kLoop, calls=%fused_computation | loop fusion | flops 1572864 | bytes 6291456 | tf_op jit(solution)/shard_map/add | solution.py:571
  117.8 1.0 copy.7
Async XLA Ops:
  0.6 115.5 %copy-start = (f32[128,4096]{1,0:T(8,128)S(1)}, f32[128,4096]{1,0:T(8,128)}, u32[]{:S(2)}) copy-start(f32[128,4096]{1,0:T(8,128)} %param.5) | copy-start | bytes 6291460

commit v4 on v3

--- a/solution.py
+++ b/solution.py
@@ -120,14 +120,15 @@
     started = []
     count = [0]
 
-    def to(src, dst, target):
+    def to(src, dst, target, start=True):
         i = count[0]
         count[0] += 1
         copy = pltpu.make_async_remote_copy(
             src_ref=src, dst_ref=dst, send_sem=ssem.at[i], recv_sem=rsem.at[i],
             device_id={"dp": target}, device_id_type=MESH,
         )
-        copy.start()
+        if start:
+            copy.start()
         started.append(copy)
         return copy
 
@@ -143,16 +144,28 @@
         ),
     ]
 
-    def meet():
-        barrier = pltpu.get_barrier_semaphore()
-
-        for target in [mate, x_to, y_to] + [
-            device(over(g), y, x, (core + h) % 2) for g in range(1, far) for h in range(2)
-        ]:
+    barrier = pltpu.get_barrier_semaphore()
+
+    def greet(targets):
+        for target in targets:
             pl.semaphore_signal(barrier, inc=1, device_id={"dp": target}, device_id_type=MESH)
+
+    def meet_plane():
+        greet([mate, x_to, y_to])
         for copy in own_copies:
             copy.start()
-        pl.semaphore_wait(barrier, 2 * far + 1)
+        pl.semaphore_wait(barrier, 3 + z)
+        greet([device(over(g), y, x, core) for g in range(1, far)])
+
+    t_copies = []
+
+    def meet_line():
+        @pl.when(z < far - 1)
+        def _():
+            pl.semaphore_wait(barrier, far - 1 - z)
+
+        for copy in t_copies:
+            copy.start()
 
     def swap_grads():
         there = 1 - core
@@ -171,7 +184,8 @@
 
     def swap_tests():
         return [
-            to(t_hbm, tbuf.at[:, pl.ds(2 * g * w, w)], device(over(g), y, x, core)) for g in (1, 2)
+            to(t_hbm, tbuf.at[:, pl.ds(2 * g * w, w)], device(over(g), y, x, core), False)
+            for g in (1, 2)
         ]
 
     def swap_factor(*groups):
@@ -489,19 +503,21 @@
 
             when_sent(e, sent)
 
-    meet()
+    meet_plane()
     swapped = swap_grads()
-    t_copies = swap_tests()
+    t_copies += swap_tests()
+    pl.when(z >= far // 2)(meet_line)
     own_copies[0].wait()
     grads_here(swapped[: half // 2 + 2])
-    early = swap_factor(0, 3, 2, 1)
     compute(3, 0, 1)
     first(3, 1)
-    relayed = relay_tests(t_copies)
+    pl.when(z < far // 2)(meet_line)
     grads_here(swapped[half // 2 + 2 :])
     compute(3, 1, 3)
     first(3, 0)
     compute(3, 3, 4)
+    relayed = relay_tests(t_copies)
+    early = swap_factor(0, 3, 2, 1)
     compute(2)
     first(2, 1)
     early += hand_tests(t_copies)
@@ -509,22 +525,22 @@
     first(2, 0)
     early += hand_relayed(relayed)
     compute(1)
+    first(1, 1)
     c_first()
     third(3)
     precondition(early)
-    first(1, 1)
     precondition_second()
     second(2)
     first(1, 0)
     compute(0)
     c_second()
+    first(0, 1)
     along_z = gather_first()
+    second(1)
+    relayed = gather_relay(along_z)
     third(2)
-    first(0, 1)
-    second(1)
+    first(0, 0)
     c_third()
-    first(0, 0)
-    relayed = gather_relay(along_z)
     second(0)
     c_fourth()
     gx, gy, mate_own = gather_second(along_z, relayed)

time: 119 us -> 117 us (0.983)
  Pallas kernels: 115 us -> 113 us
    pallas_call x1, Pallas kernels: 115 us -> 113 us  [window(): pl.pallas_call(functools.partial(kernel, s, list(scratch)), out_shape=(ja...]
where the time goes in v4:
time: 117 us; the launch traced here: 116 us
  Pallas kernels  113 us (97%)
  other arithmetic  1.65 us (1%)
    pallas_call x1, Pallas kernels, window(): pl.pallas_call(functools.partial(kernel, s, list(scratch)), out_shape=(ja...  113 us

profile of v4, /device:TPU:0, one launch (start us, length us, event | category | flops | bytes accessed | tf_op | source)
XLA Modules:
  0.0 116.0 jit_solution(7397283319675152567)
XLA Ops:
  0.6 0.0 copy-start
  0.6 112.7 %shard_map.59 = (f32[128,4096]{1,0:T(8,128)S(1)}, f32[512,512]{1,0:T(8,128)S(1)}) custom-call(bf16[512,4096]{1,0:T(8,128)(2,1)} %g_hbm.1, bf16[512,128]{1,0:T(8,128)(2,1)} %t_hbm.1, bf16[128,4096]{1,0:T(8,128)(2,1)} %f_hbm.1), custom_call_target="tpu_custom_call" | custom-call | tf_op jit(solution)/shard_map/pallas_call | solution.py:571
  113.4 0.0 copy-done
  113.4 1.6 %multiply_add_fusion = f32[128,4096]{1,0:T(8,128)} fusion(f32[128,4096]{1,0:T(8,128)S(1)} %get-tuple-element.5, f32[128,4096]{1,0:T(8,128)S(1)} %copy-done), kind=kLoop, calls=%fused_computation | loop fusion | flops 1572864 | bytes 6291456 | tf_op jit(solution)/shard_map/add | solution.py:587
  115.0 1.0 copy.7
Async XLA Ops:
  0.6 112.7 %copy-start = (f32[128,4096]{1,0:T(8,128)S(1)}, f32[128,4096]{1,0:T(8,128)}, u32[]{:S(2)}) copy-start(f32[128,4096]{1,0:T(8,128)} %param.5) | copy-start | bytes 6291460

commit v5 on v4

--- a/solution.py
+++ b/solution.py
@@ -39,7 +39,9 @@
         self.half = self.chips // 2
         self.each = self.half // 2
         self.strip = self.each * self.W + self.w // 2
-        self.rc = self.w // 2
+        self.rc = 3 * self.w // 4
+        self.hc = self.rc // 2
+        self.hs = self.hc - self.w // 4
         self.ra = (self.strip - self.rc) // 2
         self.rb = self.ra
         self.mh = tests // 2
@@ -66,15 +68,16 @@
             out_bz=v((far1, self.rb, W), BF16),
             in_az=v((far1, self.ra, W), BF16),
             in_bz=v((far1, self.rb, W), BF16),
-            part_c=v((2, 4, self.rc, W), F32),
-            out_c1=v((2, 4, self.rc, W), BF16),
-            in_c1=v((2, 4, self.rc, W), BF16),
-            out_c2=v((4, self.rc, W), BF16),
-            in_c2=v((4, self.rc, W), BF16),
-            out_c3=v((2, 2, self.rc // 2, W), BF16),
-            in_c3=v((2, 2, self.rc // 2, W), BF16),
-            out_c4=v((2, self.rc // 2, W), BF16),
-            in_c4=v((2, self.rc // 2, W), BF16),
+            part_c=v((2, 2, 4, self.hc, W), F32),
+            out_c1=v((2, 2, 4, self.hc, W), BF16),
+            in_c1=v((2, 2, 4, self.hc, W), BF16),
+            out_c2=v((2, 4, self.hc, W), BF16),
+            in_c2=v((2, 4, self.hc, W), BF16),
+            out_c3=v((2, 2, self.hc, W), BF16),
+            in_c3=v((2, 2, self.hc, W), BF16),
+            out_c4=v((2, self.hc, W), BF16),
+            in_c4=v((2, self.hc, W), BF16),
+            extra=v((w, w), F32),
             fbuf=v((2 * far * w, 4 * w), BF16),
             tbuf=v((tests, 2 * far * w), BF16),
             pp=v((tests, 4 * w), F32),
@@ -88,21 +91,21 @@
             xrecv=v((w, w), BF16),
             dsend=v((w, self.each * W), BF16),
             drecv=v((w, self.each * W), BF16),
-            ssem=pltpu.SemaphoreType.DMA((self.slots(),)),
-            rsem=pltpu.SemaphoreType.DMA((self.slots(),)),
+            ssem=pltpu.SemaphoreType.DMA((self.sends,)),
+            rsem=pltpu.SemaphoreType.DMA((self.receipts,)),
             msem=pltpu.SemaphoreType.DMA((2 * self.each,)),
             mrsem=pltpu.SemaphoreType.DMA((self.half,)),
             lsem=pltpu.SemaphoreType.DMA((4,)),
         )
 
-    def slots(self):
-        return 72 + self.chips
+    sends, receipts = 43, 68
 
 
 def kernel(s, names, g_hbm, t_hbm, f_hbm, term_ref, scores_ref, *refs):
     r = dict(zip(names, refs))
     n, far, w, W, chips, half, each = s.n, s.far, s.w, s.W, s.chips, s.half, s.each
-    rows, mh, ra, rb = s.rows, s.mh, s.ra, s.rb
+    rows, mh, ra, rb, hc, hs = s.rows, s.mh, s.ra, s.rb, s.hc, s.hs
+    mid = ra + rb + hc
     me = lax.axis_index("dp")
     core, x, y, z = me % 2, me // 2 % 2, me // 4 % 2, me // 8
     q = me // 2
@@ -118,19 +121,58 @@
     y_to = device(z, 1 - y, x, core)
     ssem, rsem = r["ssem"], r["rsem"]
     started = []
-    count = [0]
-
-    def to(src, dst, target, start=True):
-        i = count[0]
-        count[0] += 1
+    count = [0, 0]
+    shared = [{}, {}]
+
+    def slot(kind, name):
+        if name in shared[kind]:
+            return shared[kind][name]
+        i = count[kind]
+        count[kind] += 1
+        if name:
+            shared[kind][name] = i
+        return i
+
+    def to(src, dst, target, start=True, sent=None, came=None):
         copy = pltpu.make_async_remote_copy(
-            src_ref=src, dst_ref=dst, send_sem=ssem.at[i], recv_sem=rsem.at[i],
-            device_id={"dp": target}, device_id_type=MESH,
+            src_ref=src, dst_ref=dst, send_sem=ssem.at[slot(0, sent)],
+            recv_sem=rsem.at[slot(1, came)], device_id={"dp": target}, device_id_type=MESH,
         )
         if start:
             copy.start()
-        started.append(copy)
+        if not sent:
+            started.append(copy)
         return copy
+
+    def bytes_of(ref, sent=None, came=None):
+        return pltpu.make_async_remote_copy(
+            src_ref=ref, dst_ref=ref, send_sem=ssem.at[shared[0][sent] if sent else 0],
+            recv_sem=rsem.at[shared[1][came] if came else 0],
+            device_id={"dp": mate}, device_id_type=MESH,
+        )
+
+    class Either:
+        def __init__(self, src, dst, small, target):
+            i, j = slot(0, None), slot(1, None)
+            self.copies = [
+                pltpu.make_async_remote_copy(
+                    src_ref=a, dst_ref=b, send_sem=ssem.at[i], recv_sem=rsem.at[j],
+                    device_id={"dp": target}, device_id_type=MESH,
+                )
+                for a, b in ((src.at[small], dst.at[small]), (src, dst))
+            ]
+            started.append(self)
+            self.each(lambda copy: copy.start())
+
+        def each(self, act):
+            for i in range(2):
+                pl.when(core == i)(functools.partial(act, self.copies[i]))
+
+        def wait_recv(self):
+            self.each(lambda copy: copy.wait_recv())
+
+        def wait_send(self):
+            self.each(lambda copy: copy.wait_send())
 
     def lanes(block, width):
         return pl.ds(pl.multiple_of(block * width, width), width)
@@ -167,6 +209,8 @@
         for copy in t_copies:
             copy.start()
 
+    soon = half // 2 + 2
+
     def swap_grads():
         there = 1 - core
         begin = (over(3) * 2 + 1 - y) * 2 + 1 - x
@@ -175,9 +219,11 @@
         steps += [half - last * there, last + last * there]
         steps += [i - last * there for i in range(last + 1, half)] + list(range(half + 1, chips))
         parts = [lanes((begin + i) % chips, W) for i in steps]
-        return [
-            to(g_hbm.at[:, part], gbuf.at[pl.ds(rows, rows), part], mate) for part in parts
-        ]
+        for i, part in enumerate(parts):
+            to(
+                g_hbm.at[:, part], gbuf.at[pl.ds(rows, rows), part], mate,
+                sent="g", came="g0" if i < soon else "g1",
+            )
 
     def hand(g, target, came):
         return to(tbuf.at[:, pl.ds(2 * g * w, w)], tbuf.at[:, pl.ds(came * w, w)], target)
@@ -194,6 +240,7 @@
                 f_hbm.at[:, lanes((core + h) % 2 * far + over(g), 4 * w)],
                 fbuf.at[pl.ds((2 * g + h) * w, w)],
                 device(over(g), y, x, (core + h) % 2),
+                sent="f", came="f",
             )
             for g in groups
             for h in range(2)
@@ -213,7 +260,7 @@
         copy.wait_recv()
         return [hand(3, mate, 7)]
 
-    def grads_here(copies):
+    def arrived(copies):
         for copy in copies:
             copy.wait_recv()
 
@@ -239,8 +286,17 @@
                 gt[pl.ds(pl.multiple_of(core * w, w), w), :], gbuf[:, lanes(col, w)],
                 preferred_element_type=F32,
             )
-            tmp[each * W :, :w] = extra[: w // 2]
-            tmp[each * W :, w:] = extra[w // 2 :]
+
+            @pl.when(core == 0)
+            def _():
+                tmp[w:W, :w] = extra
+                tmp[mid : mid + hs] = tmp[each * W - hs : each * W]
+
+            @pl.when(core == 1)
+            def _():
+                tmp[each * W :, :w] = extra[: w // 2]
+                tmp[each * W :, w:] = extra[w // 2 :]
+
 
             @pl.when(ox == 0)
             def _():
@@ -258,10 +314,12 @@
             def _():
                 out_b1[g, ox] = tmp[ra : ra + rb].astype(BF16)
 
-            if g % 2:
-                out_c1[g // 2, 3 - i] = tmp[ra + rb :].astype(BF16)
-            else:
-                part_c[g // 2, 3 - i] = tmp[ra + rb :]
+            for h in range(2):
+                ends = tmp[ra + rb + h * hc : ra + rb + (h + 1) * hc]
+                if g % 2:
+                    out_c1[g // 2, h, 3 - i] = ends.astype(BF16)
+                else:
+                    part_c[g // 2, h, 3 - i] = ends
             return carry
 
         lax.fori_loop(first, last, strip, 0)
@@ -269,16 +327,16 @@
     a1, b1, a2, b2, az, bz = {}, {}, {}, {}, {}, {}
 
     def first(g, o):
-        a1[g, o] = to(out_a1.at[g, o], r["in_a1"].at[g, o], x_to)
-        b1[g, o] = to(out_b1.at[g, o], r["in_b1"].at[g, o], y_to)
+        a1[g, o] = to(out_a1.at[g, o], r["in_a1"].at[g, o], x_to, sent="a1")
+        b1[g, o] = to(out_b1.at[g, o], r["in_b1"].at[g, o], y_to, sent="b1")
 
     def second(g):
         a1[g, 1].wait_recv()
         r["out_a2"][g] = (part_a[g, 1] + r["in_a1"][g, 1].astype(F32)).astype(BF16)
-        a2[g] = to(r["out_a2"].at[g], r["in_a2"].at[g], y_to)
+        a2[g] = to(r["out_a2"].at[g], r["in_a2"].at[g], y_to, sent="a2")
         b1[g, 1].wait_recv()
         r["out_b2"][g] = (part_b[g, 1] + r["in_b1"][g, 1].astype(F32)).astype(BF16)
-        b2[g] = to(r["out_b2"].at[g], r["in_b2"].at[g], x_to)
+        b2[g] = to(r["out_b2"].at[g], r["in_b2"].at[g], x_to, sent="b2")
 
     def third(g):
         a1[g, 0].wait_recv()
@@ -297,41 +355,44 @@
             bz[3].wait_recv()
             total_b = total_b + r["in_bz"][2].astype(F32)
         target = device(over(2 if g == 2 else 1), y, x, core)
-        slot = {3: 2, 2: 1, 1: 0}[g]
-        r["out_az"][slot] = total_a.astype(BF16)
-        az[g] = to(r["out_az"].at[slot], r["in_az"].at[slot], target)
-        r["out_bz"][slot] = total_b.astype(BF16)
-        bz[g] = to(r["out_bz"].at[slot], r["in_bz"].at[slot], target)
+        at = {3: 2, 2: 1, 1: 0}[g]
+        r["out_az"][at] = total_a.astype(BF16)
+        az[g] = to(r["out_az"].at[at], r["in_az"].at[at], target, sent="az")
+        r["out_bz"][at] = total_b.astype(BF16)
+        bz[g] = to(r["out_bz"].at[at], r["in_bz"].at[at], target, sent="bz")
 
     c1, c2, c3, c4 = {}, [], {}, {}
-    hc = s.rc // 2
+    few = pl.ds(0, hs)
 
     def c_first():
-        for slot in (1, 0):
-            c1[slot] = to(out_c1.at[slot], in_c1.at[slot], device(over(1), y, x, core))
+        for at in (1, 0):
+            c1[at] = Either(
+                out_c1.at[at], in_c1.at[at], (slice(None), slice(None), few),
+                device(over(1), y, x, core),
+            )
 
     def c_second():
         c1[1].wait_recv()
         out_c2[...] = (part_c[1] + in_c1[1].astype(F32)).astype(BF16)
-        c2.append(to(out_c2, in_c2, device(over(2), y, x, core)))
+        c2.append(
+            Either(out_c2, in_c2, (slice(None), slice(None), few), device(over(2), y, x, core))
+        )
 
     def c_third():
         c1[0].wait_recv()
         c2[0].wait_recv()
         part_c[0] = part_c[0] + in_c1[0].astype(F32) + in_c2[...].astype(F32)
         for o in range(2):
-            out_c3[0, o] = part_c[0, 2 * o + 1, :hc].astype(BF16)
-            out_c3[1, o] = part_c[0, 2 + o, hc:].astype(BF16)
-        c3[0] = to(out_c3.at[0], in_c3.at[0], x_to)
-        c3[1] = to(out_c3.at[1], in_c3.at[1], y_to)
+            out_c3[0, o] = part_c[0, 0, 2 * o + 1].astype(BF16)
+            out_c3[1, o] = part_c[0, 1, 2 + o].astype(BF16)
+        for h, target in ((0, x_to), (1, y_to)):
+            c3[h] = Either(out_c3.at[h], in_c3.at[h], (slice(None), few), target)
 
     def c_fourth():
-        c3[0].wait_recv()
-        out_c4[0] = (part_c[0, 2, :hc] + in_c3[0, 1].astype(F32)).astype(BF16)
-        c4[0] = to(out_c4.at[0], in_c4.at[0], y_to)
-        c3[1].wait_recv()
-        out_c4[1] = (part_c[0, 1, hc:] + in_c3[1, 1].astype(F32)).astype(BF16)
-        c4[1] = to(out_c4.at[1], in_c4.at[1], x_to)
+        for h, target in ((0, y_to), (1, x_to)):
+            c3[h].wait_recv()
+            out_c4[h] = (part_c[0, h, 2 - h] + in_c3[h, 1].astype(F32)).astype(BF16)
+            c4[h] = Either(out_c4.at[h], in_c4.at[h], (few,), target)
 
     pp, in_p1, out_p2, in_p2, pfull = r["pp"], r["in_p1"], r["out_p2"], r["in_p2"], r["pfull"]
     sub = lambda oy, ox: (y + oy) % 2 * 2 + (x + ox) % 2
@@ -339,6 +400,7 @@
 
     def precondition(handed):
         own_copies[2].wait()
+        bytes_of(fbuf.at[pl.ds(0, (2 * far - 1) * w)], came="f").wait_recv()
         for copy in handed:
             copy.wait_recv()
         pp[...] = jnp.dot(tbuf[...], fbuf[...], preferred_element_type=F32)
@@ -444,13 +506,23 @@
             tmp[at : at + size] = sums[0, 0] + came[0].astype(F32) + came[1].astype(F32)
         else:
             at, size = ra + rb, s.rc
-            for i in range(2):
-                c4[i].wait_recv()
-                tmp[at + i * hc : at + (i + 1) * hc] = (
-                    part_c[0, 0, i * hc : (i + 1) * hc]
-                    + in_c3[i, 0].astype(F32)
-                    + in_c4[i].astype(F32)
+            for h in range(2):
+                c4[h].wait_recv()
+                tmp[at + h * hc : at + (h + 1) * hc] = (
+                    part_c[0, h, 0] + in_c3[h, 0].astype(F32) + in_c4[h].astype(F32)
                 )
+            extra = r["extra"]
+
+            @pl.when(core == 0)
+            def _():
+                tmp[each * W - hs : each * W] = tmp[mid : mid + hs]
+                extra[...] = tmp[w:W, :w]
+
+            @pl.when(core == 1)
+            def _():
+                extra[: w // 2] = tmp[each * W :, :w]
+                extra[w // 2 :] = tmp[each * W :, w:]
+
         for e in range(each):
             if not at < (e + 1) * W <= at + size:
                 continue
@@ -465,13 +537,18 @@
             term_ref[:, where] = tmp[pl.ds(pl.multiple_of(e * W + core * w, w), w), :]
             other = pl.ds(pl.multiple_of(e * W + (1 - core) * w, w), w)
             dsend[:, e * W : (e + 1) * W] = tmp[other, :].astype(BF16)
+            if e == 0:
+
+                @pl.when(core == 0)
+                def _():
+                    dsend[:, :w] = tmp[:w, w:W].T.astype(BF16)
+
         if part < 2:
             return None
         direct = to(dsend, drecv, mate)
-        extra = jnp.concatenate([tmp[each * W :, :w], tmp[each * W :, w:]], axis=0)
         col = 2 * ((q + half) % chips) + (core + q // half) % 2
-        term_ref[:, lanes(col, w)] = extra
-        xsend[...] = extra.T.astype(BF16)
+        term_ref[:, lanes(col, w)] = extra[...]
+        xsend[...] = extra[...].T.astype(BF16)
         mirrored = to(xsend, xrecv, col)
         return direct, mirrored
 
@@ -492,9 +569,13 @@
         term_ref[:, lanes(col, w)] = xrecv[...].astype(F32)
 
     def wait_sends():
-        assert count[0] == s.slots()
+        assert count == [s.sends, s.receipts]
         for copy in started:
             copy.wait_send()
+        for name in ("a1", "b1", "a2", "b2", "az", "bz"):
+            bytes_of(r["out_" + name], sent=name).wait_send()
+        bytes_of(g_hbm, sent="g").wait_send()
+        bytes_of(fbuf.at[pl.ds(0, (2 * far - 1) * w)], sent="f").wait_send()
         for e in range(each):
 
             def sent(e=e):
@@ -504,27 +585,28 @@
             when_sent(e, sent)
 
     meet_plane()
-    swapped = swap_grads()
+    swap_grads()
     t_copies += swap_tests()
     pl.when(z >= far // 2)(meet_line)
     own_copies[0].wait()
-    grads_here(swapped[: half // 2 + 2])
+    bytes_of(gbuf.at[pl.ds(rows, rows), pl.ds(0, soon * W)], came="g0").wait_recv()
     compute(3, 0, 1)
     first(3, 1)
     pl.when(z < far // 2)(meet_line)
-    grads_here(swapped[half // 2 + 2 :])
+    swap_factor(0, 3)
+    bytes_of(gbuf.at[pl.ds(rows, rows), pl.ds(soon * W, s.k - soon * W)], came="g1").wait_recv()
     compute(3, 1, 3)
     first(3, 0)
     compute(3, 3, 4)
-    relayed = relay_tests(t_copies)
-    early = swap_factor(0, 3, 2, 1)
     compute(2)
     first(2, 1)
-    early += hand_tests(t_copies)
     second(3)
     first(2, 0)
+    relayed = relay_tests(t_copies)
+    swap_factor(2, 1)
+    early = hand_tests(t_copies)
+    compute(1)
     early += hand_relayed(relayed)
-    compute(1)
     first(1, 1)
     c_first()
     third(3)
@@ -539,12 +621,12 @@
     second(1)
     relayed = gather_relay(along_z)
     third(2)
+    c_third()
     first(0, 0)
-    c_third()
     second(0)
+    third(1)
+    gx, gy, mate_own = gather_second(along_z, relayed)
     c_fourth()
-    gx, gy, mate_own = gather_second(along_z, relayed)
-    third(1)
     scores_start()
     score(0, 0, 1)
     third(0)
@@ -554,11 +636,11 @@
     direct, mirrored = finish(2)
     mates = gather_mates(gx, gy)
     score(0, 1, 3)
-    grads_here([mate_own] + mates)
+    arrived([mate_own] + mates)
     score(1, 0, 3)
     mate_diagonal = gather_fourth(diagonal)
     score(0, 3, 4)
-    grads_here([mate_diagonal])
+    arrived([mate_diagonal])
     score(1, 3, 4)
     close(direct, mirrored)
     wait_sends()

time: 117 us -> 114 us (0.974)
  Pallas kernels: 113 us -> 110 us
    pallas_call x1, Pallas kernels: 113 us -> 110 us  [window(): pl.pallas_call(functools.partial(kernel, s, list(scratch)), out_shape=(ja...]
where the time goes in v5:
time: 114 us; the launch traced here: 113 us
  Pallas kernels  110 us (96%)
  other arithmetic  1.65 us (1%)
    pallas_call x1, Pallas kernels, window(): pl.pallas_call(functools.partial(kernel, s, list(scratch)), out_shape=(ja...  110 us

profile of v5, /device:TPU:0, one launch (start us, length us, event | category | flops | bytes accessed | tf_op | source)
XLA Modules:
  0.0 113.5 jit_solution(4331423408857717576)
XLA Ops:
  0.6 0.0 copy-start
  0.6 110.2 %shard_map.59 = (f32[128,4096]{1,0:T(8,128)S(1)}, f32[512,512]{1,0:T(8,128)S(1)}) custom-call(bf16[512,4096]{1,0:T(8,128)(2,1)} %g_hbm.1, bf16[512,128]{1,0:T(8,128)(2,1)} %t_hbm.1, bf16[128,4096]{1,0:T(8,128)(2,1)} %f_hbm.1), custom_call_target="tpu_custom_call" | custom-call | tf_op jit(solution)/shard_map/pallas_call | solution.py:653
  110.9 0.0 copy-done
  110.9 1.6 %multiply_add_fusion = f32[128,4096]{1,0:T(8,128)} fusion(f32[128,4096]{1,0:T(8,128)S(1)} %get-tuple-element.5, f32[128,4096]{1,0:T(8,128)S(1)} %copy-done), kind=kLoop, calls=%fused_computation | loop fusion | flops 1572864 | bytes 6291456 | tf_op jit(solution)/shard_map/add | solution.py:669
  112.5 1.0 copy.7
Async XLA Ops:
  0.6 110.2 %copy-start = (f32[128,4096]{1,0:T(8,128)S(1)}, f32[128,4096]{1,0:T(8,128)}, u32[]{:S(2)}) copy-start(f32[128,4096]{1,0:T(8,128)} %param.5) | copy-start | bytes 6291460

commit v6 on v5

--- a/solution.py
+++ b/solution.py
@@ -39,7 +39,7 @@
         self.half = self.chips // 2
         self.each = self.half // 2
         self.strip = self.each * self.W + self.w // 2
-        self.rc = 3 * self.w // 4
+        self.rc = self.w
         self.hc = self.rc // 2
         self.hs = self.hc - self.w // 4
         self.ra = (self.strip - self.rc) // 2
@@ -619,14 +619,14 @@
     first(0, 1)
     along_z = gather_first()
     second(1)
+    first(0, 0)
     relayed = gather_relay(along_z)
     third(2)
     c_third()
-    first(0, 0)
     second(0)
     third(1)
+    c_fourth()
     gx, gy, mate_own = gather_second(along_z, relayed)
-    c_fourth()
     scores_start()
     score(0, 0, 1)
     third(0)
@@ -666,7 +666,38 @@
             collective_id=0, has_side_effects=True, vmem_limit_bytes=49 * 1024 * 1024
         ),
     )(*(pltpu.with_memory_space_constraint(a, pltpu.HBM) for a in (grads, test_grads, inverse_factor)))
-    return scores, 0.9 * covariance + term / (rows * n)
+    here = pl.BlockSpec(memory_space=pltpu.VMEM)
+    there = pl.BlockSpec(memory_space=pl.ANY)
+    return pl.pallas_call(
+        functools.partial(ending, rows * n),
+        out_shape=(
+            jax.ShapeDtypeStruct(scores.shape, F32),
+            jax.ShapeDtypeStruct(covariance.shape, F32),
+        ),
+        in_specs=[here, here, here],
+        out_specs=(there, there),
+        scratch_shapes=[
+            pltpu.VMEM(covariance.shape, F32),
+            pltpu.SemaphoreType.DMA((PIECES + 1,)),
+        ],
+        compiler_params=pltpu.CompilerParams(vmem_limit_bytes=8 * 1024 * 1024),
+    )(scores, term, covariance)
+
+
+PIECES = 4
+
+
+def ending(examples, scores_ref, term_ref, before_ref, scores_out, after_out, after, sem):
+    copies = [pltpu.make_async_copy(scores_ref, scores_out, sem.at[PIECES])]
+    copies[0].start()
+    piece = after.shape[0] // PIECES
+    for i in range(PIECES):
+        part = pl.ds(i * piece, piece)
+        after[part] = 0.9 * before_ref[part] + term_ref[part] / examples
+        copies.append(pltpu.make_async_copy(after.at[part], after_out.at[part], sem.at[i]))
+        copies[-1].start()
+    for copy in copies:
+        copy.wait()
 
 
 def solution(mesh):

time: 114 us -> 111 us (0.974)
  other arithmetic: 1.65 us -> 0 us
    pallas_call x1, Pallas kernels: 110 us -> 108 us  [window(): pl.pallas_call(functools.partial(kernel, s, list(scratch)), out_shape=(ja...]
    pallas_call x0 -> x1, Pallas kernels: none -> 1.7 us  [window(): pl.pallas_call(functools.partial(ending, rows * n), out_shape=(jax.ShapeD...]
    add x1 -> x0, other arithmetic: 1.65 us -> none  [window(): return (scores, 0.9 * covariance + term / (rows * n))]
where the time goes in v6:
time: 111 us
  Pallas kernels  110 us (99%)
    pallas_call x1, Pallas kernels, window(): pl.pallas_call(functools.partial(kernel, s, list(scratch)), out_shape=(ja...  108 us

profile of v6, /device:TPU:0, one launch (start us, length us, event | category | flops | bytes accessed | tf_op | source)
XLA Modules:
  0.0 110.8 jit_solution(1948333676430427335)
XLA Ops:
  0.6 0.0 copy-start
  0.6 108.4 %shard_map.59 = (f32[128,4096]{1,0:T(8,128)S(1)}, f32[512,512]{1,0:T(8,128)S(1)}) custom-call(bf16[512,4096]{1,0:T(8,128)(2,1)} %g_hbm.1, bf16[512,128]{1,0:T(8,128)(2,1)} %t_hbm.1, bf16[128,4096]{1,0:T(8,128)(2,1)} %f_hbm.1), custom_call_target="tpu_custom_call" | custom-call | tf_op jit(solution)/shard_map/pallas_call | solution.py:653
  109.1 0.0 copy-done
  109.1 1.7 %shard_map.60 = (f32[512,512]{1,0:T(8,128)}, f32[128,4096]{1,0:T(8,128)}) custom-call(f32[512,512]{1,0:T(8,128)S(1)} %get-tuple-element.4.scores_ref, f32[128,4096]{1,0:T(8,128)S(1)} %get-tuple-element.5.term_ref, f32[128,4096]{1,0:T(8,128)S(1)} %copy-done), custom_call_target="tpu_custom_call" | custom-call | tf_op jit(solution)/shard_map/pallas_call | solution.py:671
Async XLA Ops:
  0.6 108.4 %copy-start = (f32[128,4096]{1,0:T(8,128)S(1)}, f32[128,4096]{1,0:T(8,128)}, u32[]{:S(2)}) copy-start(f32[128,4096]{1,0:T(8,128)} %before_ref.1) | copy-start | bytes 6291460

commit v7 on v6

--- a/solution.py
+++ b/solution.py
@@ -94,7 +94,7 @@
             ssem=pltpu.SemaphoreType.DMA((self.sends,)),
             rsem=pltpu.SemaphoreType.DMA((self.receipts,)),
             msem=pltpu.SemaphoreType.DMA((2 * self.each,)),
-            mrsem=pltpu.SemaphoreType.DMA((self.half,)),
+            mrsem=pltpu.SemaphoreType.DMA((1,)),
             lsem=pltpu.SemaphoreType.DMA((4,)),
         )
 
@@ -339,27 +339,25 @@
         b2[g] = to(r["out_b2"].at[g], r["in_b2"].at[g], x_to, sent="b2")
 
     def third(g):
-        a1[g, 0].wait_recv()
-        a2[g].wait_recv()
-        total_a = part_a[g, 0] + r["in_a1"][g, 0].astype(F32) + r["in_a2"][g].astype(F32)
-        b1[g, 0].wait_recv()
-        b2[g].wait_recv()
-        total_b = part_b[g, 0] + r["in_b1"][g, 0].astype(F32) + r["in_b2"][g].astype(F32)
-        if g == 0:
-            part_a[0, 0] = total_a
-            part_b[0, 0] = total_b
-            return
-        if g == 2:
-            az[3].wait_recv()
-            total_a = total_a + r["in_az"][2].astype(F32)
-            bz[3].wait_recv()
-            total_b = total_b + r["in_bz"][2].astype(F32)
         target = device(over(2 if g == 2 else 1), y, x, core)
-        at = {3: 2, 2: 1, 1: 0}[g]
-        r["out_az"][at] = total_a.astype(BF16)
-        az[g] = to(r["out_az"].at[at], r["in_az"].at[at], target, sent="az")
-        r["out_bz"][at] = total_b.astype(BF16)
-        bz[g] = to(r["out_bz"].at[at], r["in_bz"].at[at], target, sent="bz")
+        at = {3: 2, 2: 1, 1: 0, 0: 0}[g]
+        for name, part, one, two, along in (
+            ("a", part_a, a1, a2, az), ("b", part_b, b1, b2, bz)
+        ):
+            one[g, 0].wait_recv()
+            two[g].wait_recv()
+            total = (
+                part[g, 0] + r[f"in_{name}1"][g, 0].astype(F32) + r[f"in_{name}2"][g].astype(F32)
+            )
+            if g == 0:
+                part[0, 0] = total
+                continue
+            out, came = r[f"out_{name}z"], r[f"in_{name}z"]
+            if g == 2:
+                along[3].wait_recv()
+                total = total + came[2].astype(F32)
+            out[at] = total.astype(BF16)
+            along[g] = to(out.at[at], came.at[at], target, sent=name + "z")
 
     c1, c2, c3, c4 = {}, [], {}, {}
     few = pl.ds(0, hs)
@@ -485,7 +483,7 @@
         d = core * each + e
         return pltpu.make_async_remote_copy(
             src_ref=msend.at[e, pl.ds(side * w, w)], dst_ref=mrecv.at[d],
-            send_sem=msem.at[2 * e + side], recv_sem=mrsem.at[d],
+            send_sem=msem.at[2 * e + side], recv_sem=mrsem.at[0],
             device_id={"dp": 2 * ((q + d) % chips) + side}, device_id_type=MESH,
         )
 
@@ -557,11 +555,12 @@
         for e in range(each):
             where = lanes((q + (1 - core) * each + e) % chips, W)
             term_ref[:, where] = drecv[:, e * W : (e + 1) * W].astype(F32)
+        all_of_them = mrecv.at[pl.ds(1, half - 1)]
+        pltpu.make_async_remote_copy(
+            src_ref=all_of_them, dst_ref=all_of_them, send_sem=msem.at[0], recv_sem=mrsem.at[0],
+            device_id={"dp": mate}, device_id_type=MESH,
+        ).wait_recv()
         for d in range(1, half):
-            pltpu.make_async_remote_copy(
-                src_ref=mrecv.at[d], dst_ref=mrecv.at[d], send_sem=msem.at[0], recv_sem=mrsem.at[d],
-                device_id={"dp": mate}, device_id_type=MESH,
-            ).wait_recv()
             term_ref[:, lanes((q + chips - d) % chips, W)] = mrecv[d].astype(F32)
         mirrored.wait_recv()
         far_chip = (q + half) % chips

time: 111 us -> 111 us (level)
  no operation moved by 1% of the time
where the time goes in v7:
time: 111 us
  Pallas kernels  110 us (99%)
    pallas_call x1, Pallas kernels, window(): pl.pallas_call(functools.partial(kernel, s, list(scratch)), out_shape=(ja...  108 us

profile of v7, /device:TPU:0, one launch (start us, length us, event | category | flops | bytes accessed | tf_op | source)
XLA Modules:
  0.0 110.7 jit_solution(2096164346436488348)
XLA Ops:
  0.6 0.0 copy-start
  0.6 108.3 %shard_map.59 = (f32[128,4096]{1,0:T(8,128)S(1)}, f32[512,512]{1,0:T(8,128)S(1)}) custom-call(bf16[512,4096]{1,0:T(8,128)(2,1)} %g_hbm.1, bf16[512,128]{1,0:T(8,128)(2,1)} %t_hbm.1, bf16[128,4096]{1,0:T(8,128)(2,1)} %f_hbm.1), custom_call_target="tpu_custom_call" | custom-call | tf_op jit(solution)/shard_map/pallas_call | solution.py:652
  108.9 0.0 copy-done
  109.0 1.7 %shard_map.60 = (f32[512,512]{1,0:T(8,128)}, f32[128,4096]{1,0:T(8,128)}) custom-call(f32[512,512]{1,0:T(8,128)S(1)} %get-tuple-element.4.scores_ref, f32[128,4096]{1,0:T(8,128)S(1)} %get-tuple-element.5.term_ref, f32[128,4096]{1,0:T(8,128)S(1)} %copy-done), custom_call_target="tpu_custom_call" | custom-call | tf_op jit(solution)/shard_map/pallas_call | solution.py:670
Async XLA Ops:
  0.6 108.3 %copy-start = (f32[128,4096]{1,0:T(8,128)S(1)}, f32[128,4096]{1,0:T(8,128)}, u32[]{:S(2)}) copy-start(f32[128,4096]{1,0:T(8,128)} %before_ref.1) | copy-start | bytes 6291460

commit v8 on v7

--- a/solution.py
+++ b/solution.py
@@ -42,8 +42,8 @@
         self.rc = self.w
         self.hc = self.rc // 2
         self.hs = self.hc - self.w // 4
-        self.ra = (self.strip - self.rc) // 2
-        self.rb = self.ra
+        self.ra = (self.strip - self.rc) // 2 + self.w // 8
+        self.rb = self.strip - self.rc - self.ra
         self.mh = tests // 2
 
     def scratch(self):
@@ -98,7 +98,7 @@
             lsem=pltpu.SemaphoreType.DMA((4,)),
         )
 
-    sends, receipts = 43, 68
+    sends, receipts = 43, 69
 
 
 def kernel(s, names, g_hbm, t_hbm, f_hbm, term_ref, scores_ref, *refs):
@@ -215,14 +215,14 @@
         there = 1 - core
         begin = (over(3) * 2 + 1 - y) * 2 + 1 - x
         last = half // 2
-        steps = [0] + [i + last * there for i in range(1, last)]
-        steps += [half - last * there, last + last * there]
+        steps = [0] + [i + (last - 1) * there for i in range(1, last)]
+        steps += [half - there, last + last * there]
         steps += [i - last * there for i in range(last + 1, half)] + list(range(half + 1, chips))
         parts = [lanes((begin + i) % chips, W) for i in steps]
         for i, part in enumerate(parts):
             to(
                 g_hbm.at[:, part], gbuf.at[pl.ds(rows, rows), part], mate,
-                sent="g", came="g0" if i < soon else "g1",
+                sent="g", came="g0" if i < 3 else "g1" if i < soon else "g2",
             )
 
     def hand(g, target, came):
@@ -271,32 +271,68 @@
     out_c3, in_c3, out_c4, in_c4 = r["out_c3"], r["in_c3"], r["out_c4"], r["in_c4"]
     part_a, part_b, out_a1, out_b1 = r["part_a"], r["part_b"], r["out_a1"], r["out_b1"]
 
+    def owner(g, i):
+        oy, ox = (3 - i) // 2, (3 - i) % 2
+        return oy, ox, (over(g) * 2 + (y + oy) % 2) * 2 + (x + ox) % 2
+
+    def superblocks(own, which):
+        for e in which:
+            col = (own + core * each + e) % chips
+            tmp[e * W : (e + 1) * W] = jnp.dot(
+                gt[...], gbuf[:, lanes(col, W)], preferred_element_type=F32
+            )
+
+    def last_rows(g, i, own):
+        col = 2 * ((own + half) % chips) + (core + own // half) % 2
+        extra = jnp.dot(
+            gt[pl.ds(pl.multiple_of(core * w, w), w), :], gbuf[:, lanes(col, w)],
+            preferred_element_type=F32,
+        )
+
+        @pl.when(core == 0)
+        def _():
+            tmp[w:W, :w] = extra
+            tmp[mid : mid + hs] = tmp[each * W - hs : each * W]
+
+        @pl.when(core == 1)
+        def _():
+            tmp[each * W :, :w] = extra[: w // 2]
+            tmp[each * W :, w:] = extra[w // 2 :]
+
+        for h in range(2):
+            ends = tmp[ra + rb + h * hc : ra + rb + (h + 1) * hc]
+            if g % 2:
+                out_c1[g // 2, h, 3 - i] = ends.astype(BF16)
+            else:
+                part_c[g // 2, h, 3 - i] = ends
+
+    def compute_first(g):
+        oy, ox, own = owner(g, 0)
+        bytes_of(gbuf.at[pl.ds(rows, rows), pl.ds(0, 3 * W)], came="g0").wait_recv()
+        gt[...] = gbuf[:, lanes(own, W)].T
+        superblocks(own, range(each // 2))
+        bytes_of(gbuf.at[pl.ds(rows, rows), pl.ds(0, (soon - 3) * W)], came="g1").wait_recv()
+        col = 2 * ((own + half) % chips) + core + own // half
+
+        @pl.when(core == 0)
+        def _():
+            tmp[w:W, :w] = jnp.dot(
+                gt[:w, :], gbuf[:, lanes(col, w)], preferred_element_type=F32
+            )
+
+        out_a1[g, 1] = tmp[:ra].astype(BF16)
+        a1[g, 1] = to(out_a1.at[g, 1], r["in_a1"].at[g, 1], x_to, sent="a1")
+        superblocks(own, range(each // 2, each))
+        out_b1[g, 1] = tmp[ra : ra + rb].astype(BF16)
+        b1[g, 1] = to(out_b1.at[g, 1], r["in_b1"].at[g, 1], y_to, sent="b1")
+        last_rows(g, 0, own)
+
     def compute(g, first=0, last=4):
         def strip(i, carry):
-            oy, ox = (3 - i) // 2, (3 - i) % 2
-            own = (over(g) * 2 + (y + oy) % 2) * 2 + (x + ox) % 2
+            oy, ox, own = owner(g, i)
             gt[...] = gbuf[:, lanes(own, W)].T
-            for e in range(each):
-                col = (own + core * each + e) % chips
-                tmp[e * W : (e + 1) * W] = jnp.dot(
-                    gt[...], gbuf[:, lanes(col, W)], preferred_element_type=F32
-                )
-            col = 2 * ((own + half) % chips) + (core + own // half) % 2
-            extra = jnp.dot(
-                gt[pl.ds(pl.multiple_of(core * w, w), w), :], gbuf[:, lanes(col, w)],
-                preferred_element_type=F32,
-            )
-
-            @pl.when(core == 0)
-            def _():
-                tmp[w:W, :w] = extra
-                tmp[mid : mid + hs] = tmp[each * W - hs : each * W]
-
-            @pl.when(core == 1)
-            def _():
-                tmp[each * W :, :w] = extra[: w // 2]
-                tmp[each * W :, w:] = extra[w // 2 :]
-
+            superblocks(own, range(each))
+            last_rows(g, i, own)
 
             @pl.when(ox == 0)
             def _():
@@ -314,12 +350,6 @@
             def _():
                 out_b1[g, ox] = tmp[ra : ra + rb].astype(BF16)
 
-            for h in range(2):
-                ends = tmp[ra + rb + h * hc : ra + rb + (h + 1) * hc]
-                if g % 2:
-                    out_c1[g // 2, h, 3 - i] = ends.astype(BF16)
-                else:
-                    part_c[g // 2, h, 3 - i] = ends
             return carry
 
         lax.fori_loop(first, last, strip, 0)
@@ -588,12 +618,10 @@
     t_copies += swap_tests()
     pl.when(z >= far // 2)(meet_line)
     own_copies[0].wait()
-    bytes_of(gbuf.at[pl.ds(rows, rows), pl.ds(0, soon * W)], came="g0").wait_recv()
-    compute(3, 0, 1)
-    first(3, 1)
+    compute_first(3)
     pl.when(z < far // 2)(meet_line)
     swap_factor(0, 3)
-    bytes_of(gbuf.at[pl.ds(rows, rows), pl.ds(soon * W, s.k - soon * W)], came="g1").wait_recv()
+    bytes_of(gbuf.at[pl.ds(rows, rows), pl.ds(soon * W, s.k - soon * W)], came="g2").wait_recv()
     compute(3, 1, 3)
     first(3, 0)
     compute(3, 3, 4)
@@ -614,10 +642,10 @@
     second(2)
     first(1, 0)
     compute(0)
+    first(0, 1)
     c_second()
-    first(0, 1)
+    second(1)
     along_z = gather_first()
-    second(1)
     first(0, 0)
     relayed = gather_relay(along_z)
     third(2)

time: 111 us -> 111 us (level)
  no operation moved by 1% of the time
where the time goes in v8:
time: 111 us; the launch traced here: 110 us
  Pallas kernels  109 us (98%)
    pallas_call x1, Pallas kernels, window(): pl.pallas_call(functools.partial(kernel, s, list(scratch)), out_shape=(ja...  108 us

profile of v8, /device:TPU:0, one launch (start us, length us, event | category | flops | bytes accessed | tf_op | source)
XLA Modules:
  0.0 110.0 jit_solution(8874481162044400528)
XLA Ops:
  0.6 0.0 copy-start
  0.6 107.7 %shard_map.59 = (f32[128,4096]{1,0:T(8,128)S(1)}, f32[512,512]{1,0:T(8,128)S(1)}) custom-call(bf16[512,4096]{1,0:T(8,128)(2,1)} %g_hbm.1, bf16[512,128]{1,0:T(8,128)(2,1)} %t_hbm.1, bf16[128,4096]{1,0:T(8,128)(2,1)} %f_hbm.1), custom_call_target="tpu_custom_call" | custom-call | tf_op jit(solution)/shard_map/pallas_call | solution.py:680
  108.3 0.0 copy-done
  108.3 1.7 %shard_map.60 = (f32[512,512]{1,0:T(8,128)}, f32[128,4096]{1,0:T(8,128)}) custom-call(f32[512,512]{1,0:T(8,128)S(1)} %get-tuple-element.4.scores_ref, f32[128,4096]{1,0:T(8,128)S(1)} %get-tuple-element.5.term_ref, f32[128,4096]{1,0:T(8,128)S(1)} %copy-done), custom_call_target="tpu_custom_call" | custom-call | tf_op jit(solution)/shard_map/pallas_call | solution.py:698
Async XLA Ops:
  0.6 107.7 %copy-start = (f32[128,4096]{1,0:T(8,128)S(1)}, f32[128,4096]{1,0:T(8,128)}, u32[]{:S(2)}) copy-start(f32[128,4096]{1,0:T(8,128)} %before_ref.1) | copy-start | bytes 6291460
